TPU v7x, 256 devices: a whole 4x4x8 slice. The times are simulated.
256 devices in a mesh: rep: 16 (over y_lo, x, core), blk: 16 (over z, y_hi).
Axes of the slice: x: 4, y: 4 (y_hi: 2, y_lo: 2; y = y_hi * 2 + y_lo), z: 8, core: 2. Of those that a mesh axis runs over, the one named last changes fastest.
Arguments:
- features: bfloat16 [2, 4096, 2048], P(None, 'rep'), may hold values from -0.125 to 0.125
- grad_act: bfloat16 [2, 4096, 24576], P(None, 'rep', 'blk'), may hold values from -2.5 to 2.5
- weights: bfloat16 [2048, 24576], P(None, 'blk'), may hold values from -6 to 6
- owner_slot: int32 [16, 48], P('blk'), may hold values from 0 to 47, each once within a row
- factors: float32 [16, 48, 2, 256, 256], P('blk', 'rep'), may hold values from -100 to 250, as said below
- roots: bfloat16 [16, 48, 2, 256, 256], P('blk', 'rep'), may hold values from -1 to 2, as said below
- helper_list: int32 [2, 16, 4], replicated, may hold values from 0 to 95, as said below
Outputs:
- weights_out: bfloat16 [16, 48, 256, 256], P('blk', 'rep')
- roots_out: bfloat16 [16, 48, 2, 256, 256], P('blk', 'rep')
Inputs may be any that keep to these rules, and one draw needn't show every extreme that they name: `owner_slot`: each row is a permutation of the slots of one group; slot s belongs to index s // 3 of rep. `factors`: symmetric positive definite. `roots`: Symmetric. `helper_list`: In a step every helper has exactly 4 ids, no id appears twice, and no helper has two ids of one group; a group has at most min(6, 16) of its ids in a step.
All inputs are finite; a program needn't handle non-finite values.
Results may differ from a plain program's by a relative error of at most 0.0085.
Values may be sent and summed in bfloat16 or wider, within the bound.
A program may use at most 128 MiB of HBM per device.

v0:
```python
import jax
import jax.numpy as jnp
from jax import lax
from jax.sharding import PartitionSpec as P

NEWTON = 3


RIDGE = 0.001
NORM_EPS = 1e-06
DECAY = 0.95
STEP_SIZE = 0.5


def exact_dot(first, second):
    return jnp.einsum("...ij,...jk->...ik", first, second)


def inverse_root(matrices):
    identity = jnp.eye(matrices.shape[-1], dtype=jnp.float32)
    ridged = matrices + RIDGE * identity
    norm_scale = jnp.sqrt(jnp.sum(ridged * ridged, axis=(-2, -1), keepdims=True) + NORM_EPS)
    current = ridged / norm_scale
    result = identity
    for newton_turn in range(NEWTON):
        factor = (5.0 * identity - current) / 4.0
        if newton_turn == 0:
            result = factor * norm_scale ** (-0.25)
        else:
            result = exact_dot(result, factor)
        if newton_turn + 1 < NEWTON:
            square = exact_dot(factor, factor)
            current = exact_dot(exact_dot(square, square), current)
    return result.astype(jnp.bfloat16)


def silu_slope(value):
    sigmoid = jax.nn.sigmoid(value)
    return sigmoid * (1.0 + value * (1.0 - sigmoid))


def body(features, grad_act, weights, owner_slot, factors, roots, helper_list):
    block_size = factors.shape[-1]
    owned = factors.shape[1]
    per_owner = 2 * owned
    slot_count = owner_slot.shape[1]
    token_count = features.shape[1]
    row_blocks = features.shape[2] // block_size
    col_blocks = grad_act.shape[2] // block_size
    rep_index = lax.axis_index("rep")
    blk_index = lax.axis_index("blk")
    slot_ids = jnp.arange(slot_count, dtype=jnp.int32)
    placing = owner_slot[0][None, :] == slot_ids[:, None]
    block_at = jnp.sum(jnp.where(placing, slot_ids[None, :], 0), axis=1)
    row_at = block_at // col_blocks
    column_pick = (
        (block_at % col_blocks)[:, None] == jnp.arange(col_blocks, dtype=jnp.int32)[None, :]
    ).astype(jnp.float32)
    mine = lax.dynamic_slice_in_dim(block_at, rep_index * owned, owned)
    grid = weights.reshape(row_blocks, block_size, col_blocks, block_size)
    own_weight = grid[mine // col_blocks, :, mine % col_blocks, :]
    current_factors = factors[0]
    current_roots = roots[0]
    owner_ids = blk_index * per_owner + jnp.arange(per_owner, dtype=jnp.int32)
    for step_index in range(features.shape[0]):
        features_now = features[step_index]
        feature_blocks = features_now.reshape(token_count, row_blocks, block_size)
        if step_index == 0:
            gate_value = jnp.dot(features_now, weights, preferred_element_type=jnp.float32)
        else:
            chosen = jnp.take(feature_blocks, row_at, axis=1)
            products = jnp.einsum(
                "tsa,sab->tsb",
                chosen,
                lax.all_gather(own_weight, "rep", axis=0, tiled=True),
                preferred_element_type=jnp.float32,
            )
            gate_value = jnp.einsum("tsb,sj->tjb", products, column_pick)
            gate_value = gate_value.reshape(token_count, col_blocks * block_size)
        dgate = (grad_act[step_index].astype(jnp.float32) * silu_slope(gate_value)).astype(
            jnp.bfloat16
        )
        dgate_blocks = dgate.reshape(token_count, col_blocks, block_size)
        left_rows = jnp.take(feature_blocks, block_at // col_blocks, axis=1)
        right_cols = jnp.take(dgate_blocks, block_at % col_blocks, axis=1)
        grads = lax.psum_scatter(
            jnp.einsum(
                "tsa,tsb->sab", left_rows, right_cols, preferred_element_type=jnp.float32
            ).astype(jnp.bfloat16),
            "rep",
            scatter_dimension=0,
            tiled=True,
        ).astype(jnp.float32)
        grads_low = grads.astype(jnp.bfloat16)
        left_side = jnp.einsum(
            "kij,kjl->kil", current_roots[:, 0], grads_low, preferred_element_type=jnp.float32
        ).astype(jnp.bfloat16)
        shaped = jnp.einsum(
            "kij,kjl->kil", left_side, current_roots[:, 1], preferred_element_type=jnp.float32
        )
        grad_norm = jnp.sqrt(jnp.sum(grads * grads, axis=(-2, -1), keepdims=True) + NORM_EPS)
        shaped_norm = jnp.sqrt(jnp.sum(shaped * shaped, axis=(-2, -1), keepdims=True) + NORM_EPS)
        stored_weight = lax.optimization_barrier(own_weight).astype(jnp.float32)
        own_weight = (stored_weight - STEP_SIZE * (grad_norm / shaped_norm) * shaped).astype(
            jnp.bfloat16
        )
        left_stat = exact_dot(grads, jnp.swapaxes(grads, -1, -2))
        right_stat = exact_dot(jnp.swapaxes(grads, -1, -2), grads)
        current_factors = DECAY * current_factors + (1.0 - DECAY) * jnp.stack(
            [left_stat, right_stat], axis=1
        )
        flat_factors = current_factors.reshape(per_owner, block_size, block_size)
        listing = helper_list[step_index]
        matches = listing[:, :, None] == owner_ids[None, None, :]
        sending = jnp.any(matches, axis=1).astype(jnp.float32)
        refreshed = jnp.sum(sending, axis=0)
        computed = inverse_root(flat_factors)
        previous = current_roots.reshape(per_owner, block_size, block_size)
        current_roots = jnp.where(refreshed[:, None, None] > 0.5, computed, previous).reshape(
            owned, 2, block_size, block_size
        )
    return (own_weight[None], current_roots[None])


def solution(mesh):
    return jax.shard_map(
        body,
        mesh=mesh,
        in_specs=(
            P(None, "rep", None),
            P(None, "rep", "blk"),
            P(None, "blk"),
            P("blk", None),
            P("blk", "rep", None, None, None),
            P("blk", "rep", None, None, None),
            P(),
        ),
        out_specs=(P("blk", "rep", None, None), P("blk", "rep", None, None, None)),
        check_vma=False,
    )
```

profile of v0, /device:TPU:8, one launch (start us, length us, event | category | flops | bytes accessed | tf_op | source)
XLA Modules:
  0.0 320.4 jit_solution(12098752500672347873)
XLA Ops:
  7.2 0.8 select_reduce_fusion
  8.0 1.7 fusion.168
  9.7 0.5 copy.159
  10.2 0.5 copy.125
  10.8 5.4 %fusion.46 = bf16[256,1536]{1,0:T(8,128)(2,1)S(1)} fusion(bf16[2048,1536]{1,0:T(8,128)(2,1)} %param.13, bf16[2,256,1536]{2,1,0:T(8,128)(2,1)} %param.12, bf16[2,256,2048]{2,1,0:T(8,128)(2,1)} %param.11), kind=kOutput, calls=%fused_computation.43 | convolution fusion | flops 1614544896 | bytes 8912896 | tf_op jit(solution)/shard_map/dot_general | solution.py:69
  16.2 1.2 copy.126
  17.3 1.4 copy.127
  18.7 4.9 %gather_fusion.1 = bf16[48,256,256]{2,1,0:T(8,128)(2,1)} fusion(bf16[256,8,256]{2,0,1:T(8,128)(2,1)S(1)} %copy.125, s32[1024]{0:T(1024)S(1)} %pad_clamp_fusion.1), kind=kCustom, calls=%fused_computation.clone | custom fusion | bytes 12583104 | tf_op jit(solution)/shard_map/jit(_take)/gather | solution.py:84
  23.6 4.9 %gather_fusion.2 = bf16[48,256,256]{2,1,0:T(8,128)(2,1)} fusion(bf16[256,6,256]{2,0,1:T(8,128)(2,1)S(1)} %copy.127, s32[1024]{0:T(1024)S(1)} %pad_clamp_fusion), kind=kCustom, calls=%fused_computation.1.clone | custom fusion | bytes 12583104 | tf_op jit(solution)/shard_map/jit(_take)/gather | solution.py:85
  28.5 9.8 %fusion.17 = bf16[48,256,256]{2,1,0:T(8,128)(2,1)} fusion(bf16[48,256,256]{2,1,0:T(8,128)(2,1)} %gather_fusion.2, pred[48]{0:T(512)(128)(4,1)S(1)} %get-tuple-element.19, bf16[48,256,256]{2,1,0:T(8,128)(2,1)} %gather_fusion.1, pred[48]{0:T(512)(128)(4,1)S(1)} %get-tuple-element.8), kind=kOutput, calls=%fused_computation.21 | convolution fusion | flops 1620049920 | bytes 18874464 | tf_op jit(solution)/shard_map/tsa,tsb->sab/dot_general | solution.py:87
  38.4 13.4 %reshape.265 = bf16[8,256,6,256]{3,2,1,0:T(8,128)(2,1)} reshape(bf16[2048,1536]{1,0:T(8,128)(2,1)} %param.13) | data formatting | bytes 12582912 | tf_op jit(solution)/shard_map/reshape | solution.py:60
  51.8 7.9 %copy.123 = bf16[8,256,6,256]{3,1,2,0:T(8,128)(2,1)} copy(bf16[8,256,6,256]{3,2,1,0:T(8,128)(2,1)} %reshape.265) | data formatting | bytes 12582912 | tf_op jit(solution)/shard_map/reshape | solution.py:60
  59.7 0.1 fusion.149
  59.8 3.5 %gather_fusion = bf16[3,256,256]{2,1,0:T(8,128)(2,1)S(1)} fusion(bf16[8,256,6,256]{3,1,2,0:T(8,128)(2,1)} %copy.123, s32[3]{0:T(128)S(1)} %fusion.149), kind=kCustom, calls=%fused_computation.4 | custom fusion | bytes 786456 | tf_op jit(solution)/shard_map/gather | solution.py:61
  63.3 51.0 %reduce-scatter.3.cloned.1.call-done = bf16[3,256,256]{2,1,0:T(8,128)(2,1)} async-done(((bf16[48,256,256]{2,1,0:T(8,128)(2,1)}), bf16[3,256,256]{2,1,0:T(8,128)(2,1)}) %reduce-scatter.3.cloned.1.call-update) | async-done | bytes 393232 | tf_op jit(solution)/shard_map/reduce_scatter | solution.py:86
  114.2 1.2 multiply_reduce_fusion.4
  115.4 1.6 multiply_reduce_fusion.3
  117.1 0.9 subtract_convert_fusion.1
  118.0 0.2 reduce-scatter.5.cloned.1.call-start
  118.3 0.5 copy.160
  118.8 0.5 copy.133
  119.3 4.9 %gather_fusion.3 = bf16[48,256,256]{2,1,0:T(8,128)(2,1)} fusion(bf16[256,8,256]{2,0,1:T(8,128)(2,1)S(1)} %copy.133, s32[1024]{0:T(1024)S(1)} %pad_clamp_fusion.1), kind=kCustom, calls=%fused_computation.2.clone | custom fusion | bytes 12583104 | tf_op jit(solution)/shard_map/jit(_take)/gather | solution.py:84
  124.3 0.3 copy.161
  124.6 0.3 copy.138
  124.8 37.6 %all-gather.2.cloned.1.call-done = bf16[48,256,256]{2,1,0:T(8,128)(2,1)} async-done(((bf16[3,256,256]{2,1,0:T(8,128)(2,1)}), bf16[48,256,256]{2,1,0:T(8,128)(2,1)}) %all-gather.2.cloned.1.call-update) | async-done | bytes 6291472 | tf_op jit(solution)/shard_map/all_gather | solution.py:75
  162.4 9.9 %fusion.14 = bf16[256,48,256]{0,2,1:T(8,128)(2,1)} fusion(bf16[48,256,256]{2,1,0:T(8,128)(2,1)} %all-gather.2.cloned.1.call-done, bf16[48,256,256]{2,1,0:T(8,128)(2,1)} %gather_fusion.3, pred[48]{0:T(512)(128)(4,1)S(1)} %get-tuple-element.8), kind=kOutput, calls=%fused_computation.20 | convolution fusion | flops 1613758464 | bytes 18874416 | tf_op jit(solution)/shard_map/tsa,sab->tsb/dot_general | solution.py:72
  172.3 8.9 %copy.136 = bf16[256,48,256]{2,1,0:T(8,128)(2,1)} copy(bf16[256,48,256]{0,2,1:T(8,128)(2,1)} %fusion.14) | data formatting | bytes 12582912 | tf_op jit(solution)/shard_map/tsa,sab->tsb/transpose | solution.py:72
  181.2 3.7 %fusion.144 = f32[6,256,256]{2,0,1:T(8,128)S(1)} fusion(bf16[256,48,256]{2,1,0:T(8,128)(2,1)} %copy.136, s32[48]{0:T(128)S(1)} %get-tuple-element.20), kind=kOutput, calls=%fused_computation.129 | convolution fusion | flops 37749024 | bytes 7864512 | tf_op jit(solution)/shard_map/tsb,sj->tjb/dot_general | solution.py:78
  184.9 0.8 fusion.55
  185.8 4.9 %gather_fusion.4 = bf16[48,256,256]{2,1,0:T(8,128)(2,1)} fusion(bf16[256,6,256]{2,0,1:T(8,128)(2,1)S(1)} %fusion.55, s32[1024]{0:T(1024)S(1)} %pad_clamp_fusion), kind=kCustom, calls=%fused_computation.3.clone | custom fusion | bytes 12583104 | tf_op jit(solution)/shard_map/jit(_take)/gather | solution.py:85
  190.6 9.7 %fusion.22 = bf16[48,256,256]{2,1,0:T(8,128)(2,1)} fusion(bf16[48,256,256]{2,1,0:T(8,128)(2,1)} %gather_fusion.4, pred[48]{0:T(512)(128)(4,1)S(1)} %get-tuple-element.19, bf16[48,256,256]{2,1,0:T(8,128)(2,1)} %gather_fusion.3, pred[48]{0:T(512)(128)(4,1)S(1)} %get-tuple-element.8), kind=kOutput, calls=%fused_computation.22 | convolution fusion | flops 1620049920 | bytes 18874464 | tf_op jit(solution)/shard_map/tsa,tsb->sab/dot_general | solution.py:87
  200.4 0.6 copy-done.9
  201.1 0.1 compare_reduce_fusion
  201.2 0.1 convert_reduce_fusion
  201.3 0.7 fusion.141
  202.1 0.3 fusion.169
  202.4 0.3 fusion.170
  202.7 0.2 maximum_multiply_fusion
  202.9 1.3 copy.143
  204.2 70.1 %reduce-scatter.5.cloned.1.call-done = bf16[3,256,256]{2,1,0:T(8,128)(2,1)} async-done(((bf16[48,256,256]{2,1,0:T(8,128)(2,1)}), bf16[3,256,256]{2,1,0:T(8,128)(2,1)}) %reduce-scatter.5.cloned.1.call-update) | async-done | bytes 393232 | tf_op jit(solution)/shard_map/reduce_scatter | solution.py:86
  274.2 1.6 fusion.172
  275.8 0.3 fusion.173
  276.1 0.9 fusion.45
  277.1 1.2 copy.141
  278.3 0.1 copy.144
  278.4 0.1 sqrt.54
  278.5 0.1 copy.149
  278.7 0.2 maximum_multiply_fusion.2
  278.9 0.2 copy.148
  279.1 0.5 copy-done.7
  279.6 0.7 copy-done.3
  280.3 0.5 copy-done.4
  280.8 0.5 fusion.48
  281.3 1.8 fusion.32
  283.1 2.7 fusion.174
  285.8 5.1 %fusion.29 = bf16[6,256,256]{2,1,0:T(8,128)(2,1)} fusion(f32[6,256,256]{2,1,0:T(8,128)} %fusion.174, f32[256,256]{1,0:T(8,128)S(1)} %fusion.142), kind=kOutput, calls=%fused_computation.25 | convolution fusion | flops 403439616 | bytes 2621440 | tf_op jit(solution)/shard_map/...ij,...jk->...ik/dot_general | solution.py:16
  290.9 1.8 fusion.38
  292.8 2.7 fusion.171
  295.4 5.2 %fusion.35 = bf16[6,256,256]{2,1,0:T(8,128)(2,1)} fusion(f32[6,256,256]{2,1,0:T(8,128)} %fusion.171, f32[256,256]{1,0:T(8,128)S(1)} %fusion.142), kind=kOutput, calls=%fused_computation.29 | convolution fusion | flops 403439616 | bytes 2621440 | tf_op jit(solution)/shard_map/...ij,...jk->...ik/dot_general | solution.py:16
  300.6 4.1 %fusion.103 = bf16[6,256,256]{2,1,0:T(8,128)(2,1)} fusion(bf16[6,256,256]{2,1,0:T(8,128)(2,1)} %bitcast.159, bf16[6,256,256]{2,1,0:T(8,128)(2,1)} %fusion.35, f32[6,256,256]{2,1,0:T(8,128)} %fusion.171, f32[6,256,256]{2,1,0:T(8,128)S(1)} %get-tuple-element.13, f32[6]{0:T(128)S(1)} %power_multiply_fusion.1, f32[256,256]{1,0:T(8,128)S(1)} %fusion.142, ...), kind=kOutput, calls=%fused_computation.87 | convolution fusion | flops 607125504 | bytes 5767198 | tf_op jit(solution)/shard_map/...ij,...jk->...ik/dot_general | solution.py:16
  304.7 1.3 multiply_reduce_fusion.2
  306.0 2.5 multiply_reduce_fusion.1
  308.6 3.1 fusion.98
  311.7 2.1 fusion.140
  (39 shorter events, 0.4 us)
Async XLA Ops:
  7.2 107.1 %reduce-scatter.3.cloned.1.call-start = ((), (), s32[]{:S(2)}) async-start(), calls=%async_computation.2 | async-start | bytes 6684672 | tf_op jit(solution)/shard_map/reduce_scatter | solution.py:86
  38.3 124.1 %all-gather.2.cloned.1.call-start = ((), (), s32[]{:S(2)}) async-start(), calls=%async_computation.3 | async-start | bytes 6684672 | tf_op jit(solution)/shard_map/all_gather | solution.py:75
  38.4 13.4 %copy-start.5 = (bf16[1,3,2,256,256]{4,3,2,1,0:T(8,128)(2,1)S(1)}, bf16[1,3,2,256,256]{4,3,2,1,0:T(8,128)(2,1)}, u32[]{:S(2)}) copy-start(bf16[1,3,2,256,256]{4,3,2,1,0:T(8,128)(2,1)} %param.16) | copy-start | bytes 2359300
  118.0 156.2 %reduce-scatter.5.cloned.1.call-start = ((), (), s32[]{:S(2)}) async-start(), calls=%async_computation.4 | async-start | bytes 6684672 | tf_op jit(solution)/shard_map/reduce_scatter | solution.py:86
  119.3 5.0 %slice-start = ((bf16[2,256,1536]{2,1,0:T(8,128)(2,1)}), bf16[1,256,1536]{2,1,0:T(8,128)(2,1)S(1)}, s32[]{:S(2)}) async-start(bf16[2,256,1536]{2,1,0:T(8,128)(2,1)} %param.12), calls=%async_computation.5 | async-start | bytes 1572864 | tf_op jit(solution)/shard_map/slice | solution.py:80
  200.4 0.7 copy-start.9
  200.4 1.7 copy-start
  274.2 1.6 copy-start.2
  274.2 1.9 copy-start.6
  274.2 1.9 copy-start.8
  278.7 1.0 copy-start.7
  278.9 1.4 copy-start.3
  278.9 1.9 copy-start.4
  304.7 3.9 %copy-start.1 = (f32[6,256,256]{2,1,0:T(8,128)S(1)}, f32[6,256,256]{2,1,0:T(8,128)}, u32[]{:S(2)}) copy-start(f32[6,256,256]{2,1,0:T(8,128)} %fusion.174) | copy-start | bytes 4718596
Sparse Core Ops, SparseCore 0:
  38.4 75.7 reduce-scatter.2
  118.1 44.2 all-gather.1
  200.5 73.6 reduce-scatter.4
where the time goes:
time: 322 us; the launch traced here: 320 us
  waiting for transfers between devices  159 us (49%)
  matrix products  71.7 us (22%)
  local copies, waits for them, and re-layouts  65.5 us (20%)
  between operations  14 us (4%)
  other arithmetic  10.2 us (3%)
    reduce_scatter x2, waiting for transfers between devices, body(): lax.psum_scatter(jnp.einsum('tsa,tsb->sab', left_rows, right_cols, prefer...  121 us
    all_gather x1, waiting for transfers between devices, body(): lax.all_gather(own_weight, 'rep', axis=0, tiled=True)  37.6 us
    dot_general x12, matrix products, exact_dot(): return jnp.einsum('...ij,...jk->...ik', first, second)  29 us
    reshape x2, local copies, waits for them, and re-layouts, body(): grid = weights.reshape(row_blocks, block_size, col_blocks, block_size)  21.3 us
    dot_general x2, matrix products, body(): jnp.einsum('tsa,tsb->sab', left_rows, right_cols, preferred_element_type=...  19.6 us
    dot_general x1, matrix products, body(): jnp.einsum('tsa,sab->tsb', chosen, lax.all_gather(own_weight, 'rep', axis...  9.91 us
    gather x2, local copies, waits for them, and re-layouts, body(): left_rows = jnp.take(feature_blocks, block_at // col_blocks, axis=1)  9.8 us
    gather x2, local copies, waits for them, and re-layouts, body(): right_cols = jnp.take(dgate_blocks, block_at % col_blocks, axis=1)  9.77 us
  transfers between devices with their start and end apart: 3, of which 3 were waited for; matrix products, arithmetic and copies ran while one was open for 11% of the time, Pallas kernels for 0%

commit v1 on v0

v1 whole, which is shorter than its diff:
```python
import jax
import jax.numpy as jnp
from jax import lax
from jax.experimental import pallas as pl
from jax.experimental.pallas import tpu as pltpu
from jax.sharding import PartitionSpec as P

NEWTON = 3
RIDGE = 0.001
NORM_EPS = 1e-06
DECAY = 0.95
STEP_SIZE = 0.5

B = 256
H = B // 2
OWN = 3
RB = 8
CB = 6
XN = 4
F32 = jnp.float32
BF16 = jnp.bfloat16
MESH = pl.DeviceIdType.MESH

ORDER = (
    [(2, 1, 1), (2, 1, 2), (2, 0, 1), (2, 0, 2)]
    + [(2, 1, 0), (1, 1, 0), (3, 1, 0), (0, 1, 0)]
    + [(1, 1, 2), (3, 1, 1), (1, 0, 2), (3, 0, 1)]
    + [(1, 1, 1), (3, 1, 2), (1, 0, 1), (3, 0, 2)]
    + [(2, 0, 0), (1, 0, 0), (3, 0, 0), (0, 0, 0)]
    + [(0, 1, 1), (0, 1, 2), (0, 0, 1), (0, 0, 2)]
)
PLACE = {item: q for q, item in enumerate(ORDER)}


def transfer_names():
    names = [("x", 0), ("x", 1)]
    for t in range(2):
        names += [("D", t, j) for j in range(CB)]
        names += [("s1", t, way, dy) for way in range(2) for dy in range(2)]
        names += [("a1", t, dx) for dx in range(4)]
        names += [("in", t, way, dy) for way in range(2) for dy in range(2)]
        names += [("de", t, way, dy) for way in range(2) for dy in range(2)]
        names += [(kind, t, way) for kind in ("fa", "ia", "da") for way in range(2)]
        names += [("b2", t, k) for k in (1, 2)]
    names += [(kind, k) for kind in ("yo", "r", "l") for k in range(OWN)]
    names += [(kind, k) for kind in ("rp", "lp") for k in (1, 2)]
    names += [("ya", place) for place in "LRF"]
    names += ["rh", "lh"]
    names += [(kind, dy) for kind in ("rf", "lf") for dy in range(2)]
    names += [("d",) + item for item in ORDER]
    return {name: n for n, name in enumerate(names)}


NAMES = transfer_names()


def dot(first, second):
    return jnp.dot(first, second, preferred_element_type=F32)


def low(value):
    return value.astype(BF16)


def total(value):
    return jnp.sum(value, axis=(0, 1), keepdims=True)


def kernel(
    place, owner, listing, feat, act, wts, fac, rts,
    wout, rout,
    xraw, xpeer, xt0, xt1, wbuf, actb, db0, db1, pb, wg, wown, gbuf, fbuf, qbuf,
    fwdb, froml, fromr, ya, fwda, fromla, fromra, yb,
    ssem, rsem, lsem,
):
    xt, db = (xt0, xt1), (db0, db1)
    r = lax.axis_index("rep")
    group = lax.axis_index("blk")
    c = lax.rem(r, 2)
    x = lax.rem(r // 2, XN)
    y = r // (2 * XN)

    def rep_of(yy, xx, cc):
        return (yy * XN + xx) * 2 + cc

    def right_by(dx):
        return lax.rem(x + dx, XN)

    def y_of(dy):
        return y if dy == 0 else 1 - y

    def slot(dx, dy, cc, k):
        return OWN * rep_of(y_of(dy), right_by(dx), cc) + k

    sib = rep_of(y, x, 1 - c)
    yp = rep_of(1 - y, x, c)
    xr = rep_of(y, right_by(1), c)
    xl = rep_of(y, right_by(3), c)

    def load(n, src, dst):
        copy = pltpu.make_async_copy(src, dst, lsem.at[n])
        copy.start()
        return copy

    def wait_weights(j):
        columns = wbuf.at[pl.ds(j * RB, RB)]
        pltpu.make_async_copy(columns, columns, lsem.at[j]).wait()

    load_x = [load(CB, feat.at[0], xraw.at[0])]
    for j in range(CB):
        for i in range(RB):
            load(j, wts.at[pl.ds(i * B, B), pl.ds(j * B, B)], wbuf.at[j * RB + i])
    load_a = load(CB + 1, act, actb)
    load_x.append(load(CB + 2, feat.at[1], xraw.at[1]))
    load_f = load(CB + 3, fac.at[0], fbuf)
    load_q = load(CB + 4, rts.at[0], qbuf)

    barrier = pltpu.get_barrier_semaphore()
    for partner in (sib, yp, xr, xl):
        pl.semaphore_signal(barrier, inc=1, device_id={"rep": partner}, device_id_type=MESH)
    pl.semaphore_wait(barrier, 4)

    started = []

    def remote(n, src, dst, dev):
        return pltpu.make_async_remote_copy(
            src_ref=src, dst_ref=dst, send_sem=ssem.at[n], recv_sem=rsem.at[n],
            device_id={"rep": dev}, device_id_type=MESH,
        )

    def send(name, src, dst, dev):
        copy = remote(NAMES[name], src, dst, dev)
        copy.start()
        started.append(copy)

    def arrived(name, ref, dev):
        remote(NAMES[name], ref, ref, dev).wait_recv()

    for t in range(2):
        send(("x", t), feat.at[t], xpeer.at[t], sib)

    def transpose(src, t, half):
        def turn(i, carry):
            cols = pl.ds(pl.multiple_of(i * B, B), B)
            xt[t][i, :, half * B:(half + 1) * B] = src[t, :, cols].T
            return carry
        lax.fori_loop(0, RB, turn, 0)

    def gate(t, ready):
        def one(j, carry):
            if ready is not None:
                ready(j)
            value = dot(xraw[t], wbuf[pl.ds(j * RB, RB)].reshape(RB * B, B))
            sigmoid = 1.0 / (1.0 + jnp.exp(-value))
            slope = sigmoid * (1.0 + value * (1.0 - sigmoid))
            cols = pl.ds(pl.multiple_of(j * B, B), B)
            db[t][j, 0:B, :] = low(actb[t, :, cols].astype(F32) * slope)
            remote(
                NAMES[("D", t, 0)] + j, db[t].at[j, pl.ds(0, B), :], db[t].at[j, pl.ds(B, B), :], sib
            ).start()
            return carry
        lax.fori_loop(0, CB, one, 0)
        for j in range(CB):
            own = db[t].at[j, pl.ds(0, B), :]
            other = db[t].at[j, pl.ds(B, B), :]
            started.append(remote(NAMES[("D", t, j)], own, other, sib))
            arrived(("D", t, j), other, sib)

    def partials(t, first, count):
        slots = [slot(dx, dy, c, k) for dx, dy, k in ORDER[first:first + count]]

        def one(n, carry):
            here = slots[0]
            for m in range(1, count):
                here = jnp.where(n == m, slots[m], here)
            pb[t, first + n] = low(dot(xt[t][place[0, here]], db[t][place[1, here]]))
            return carry
        lax.fori_loop(0, count, one, 0)

    def p(t, dx, dy, k):
        return pb.at[t, PLACE[(dx, dy, k)]]

    def reduce_blocks(t, between):
        side = ((xr, 1, xl), (xl, 3, xr))
        partials(t, 0, 4)
        for dy in (1, 0):
            for way in range(2):
                send(("s1", t, way, dy), p(t, 2, dy, 1 + way), fwdb.at[t, way, dy], side[way][0])
        partials(t, 4, 4)
        for dx in (2, 1, 3, 0):
            send(("a1", t, dx), p(t, dx, 1, 0), ya.at[t, dx], yp)
        partials(t, 8, 4)
        land = (froml, fromr)
        for dy in (1, 0):
            for way in range(2):
                k = 2 - way
                send(("in", t, way, dy), p(t, side[way][1], dy, k), land[way].at[t, dy, k - 1], side[way][0])
        for first in (12, 16, 20):
            partials(t, first, 4)
        between()

        def pass_on(dy):
            for way in range(2):
                k = 1 + way
                arrived(("s1", t, way, dy), fwdb.at[t, way, dy], side[way][2])
                mine = p(t, side[way][1], dy, k)
                mine[...] = low(mine[...].astype(F32) + fwdb[t, way, dy].astype(F32))
                send(("de", t, way, dy), mine, land[way].at[t, dy, k - 1], side[way][0])

        def add_y(dx):
            arrived(("a1", t, dx), ya.at[t, dx], yp)
            return p(t, dx, 0, 0)[...].astype(F32) + ya[t, dx].astype(F32)

        halves = (pl.ds(0, H), pl.ds(H, H))
        land_a = (fromla, fromra)
        pass_on(1)
        p(t, 2, 0, 0)[...] = low(add_y(2))
        for way in range(2):
            send(("fa", t, way), p(t, 2, 0, 0).at[halves[way]], fwda.at[t, way], side[way][0])
        pass_on(0)
        for way in range(2):
            dx = side[way][1]
            p(t, dx, 0, 0)[...] = low(add_y(dx))
            send(("ia", t, way), p(t, dx, 0, 0).at[halves[1 - way]], land_a[way].at[t, 1 - way], side[way][0])
        gbuf[0] = add_y(0)
        for way in range(2):
            arrived(("fa", t, way), fwda.at[t, way], side[way][2])
            mine = p(t, side[way][1], 0, 0).at[halves[way]]
            mine[...] = low(mine[...].astype(F32) + fwda[t, way].astype(F32))
            send(("da", t, way), mine, land_a[way].at[t, way], side[way][0])

        def summed(dy, k):
            for way in range(2):
                kind = "de" if k == 1 + way else "in"
                arrived((kind, t, way, dy), land[way].at[t, dy, k - 1], side[way][2])
            return (
                p(t, 0, dy, k)[...].astype(F32)
                + froml[t, dy, k - 1].astype(F32) + fromr[t, dy, k - 1].astype(F32)
            )

        for k in (1, 2):
            p(t, 0, 1, k)[...] = low(summed(1, k))
            send(("b2", t, k), p(t, 0, 1, k), yb.at[t, k - 1], yp)
        for k in (1, 2):
            gbuf[k] = summed(0, k)
        for way in range(2):
            arrived(("ia", t, way), land_a[way].at[t, 1 - way], side[way][2])
            arrived(("da", t, way), land_a[way].at[t, way], side[way][2])
        for half in range(2):
            rows = slice(half * H, (half + 1) * H)
            gbuf[0, rows, :] += fromla[t, half].astype(F32) + fromra[t, half].astype(F32)

    def finish_sum(t, k):
        if k > 0:
            arrived(("b2", t, k), yb.at[t, k - 1], yp)
            gbuf[k] = gbuf[k] + yb[t, k - 1].astype(F32)

    def update(k):
        grad = gbuf[k]
        left = low(dot(qbuf[k, 0], low(grad)))
        shaped = dot(left, qbuf[k, 1])
        grad_norm = jnp.sqrt(total(grad * grad) + NORM_EPS)
        shaped_norm = jnp.sqrt(total(shaped * shaped) + NORM_EPS)
        value = low(wown[k].astype(F32) - STEP_SIZE * (grad_norm / shaped_norm) * shaped)
        wown[k] = value
        return value

    def refresh(t, k):
        grad = low(gbuf[k])
        turned = grad.T
        rows = lax.broadcasted_iota(jnp.int32, (B, B), 0)
        cols = lax.broadcasted_iota(jnp.int32, (B, B), 1)
        diagonal = rows == cols
        five = jnp.where(diagonal, F32(5.0), F32(0.0))
        stats = (dot(grad, turned), dot(turned, grad))
        for e in range(2):
            fresh = DECAY * fbuf[k, e] + (1.0 - DECAY) * stats[e]
            fbuf[k, e] = fresh
            ridged = fresh + jnp.where(diagonal, F32(RIDGE), F32(0.0))
            scale = jnp.sqrt(total(ridged * ridged) + NORM_EPS)
            current = ridged / scale
            factor = (five - current) * 0.25
            result = factor / jnp.sqrt(jnp.sqrt(scale))
            for turn in range(1, NEWTON):
                factor_low = low(factor)
                square = low(dot(factor_low, factor_low))
                current = dot(low(dot(square, square)), low(current))
                factor = (five - current) * 0.25
                result = dot(low(result), low(factor))
            name = group * (2 * OWN) + 2 * k + e
            hits = total(jnp.where(listing[t] == name, F32(1.0), F32(0.0)))
            qbuf[k, e] = jnp.where(hits > 0.5, low(result), qbuf[k, e])

    def w_at(dx, dy, k):
        return wg.at[slot(dx, dy, c, k)]

    def share(dx, dy, k):
        ref = w_at(dx, dy, k)
        send(("d", dx, dy, k), ref, ref, sib)

    def gather_blocks():
        def ship(name, ref, dev):
            send(name, ref, ref, dev)

        for k in range(OWN):
            finish_sum(0, k)
            wg[slot(0, 0, c, k)] = update(k)
            ship(("r", k), w_at(0, 0, k), xr)
            ship(("l", k), w_at(0, 0, k), xl)
            if k > 0:
                ship(("yo", k), w_at(0, 0, k), yp)
            share(0, 0, k)
        ship(("yo", 0), w_at(0, 0, 0), yp)
        refresh(0, 0)
        top, bottom = pl.ds(0, H), pl.ds(H, H)
        arrived(("r", 0), w_at(3, 0, 0), xl)
        ship("rh", w_at(3, 0, 0).at[top], xr)
        ship(("ya", "L"), w_at(3, 0, 0), yp)
        share(3, 0, 0)
        arrived(("l", 0), w_at(1, 0, 0), xr)
        ship("lh", w_at(1, 0, 0).at[bottom], xl)
        ship(("ya", "R"), w_at(1, 0, 0), yp)
        share(1, 0, 0)
        for k in (1, 2):
            arrived(("yo", k), w_at(0, 1, k), yp)
            ship(("rp", k), w_at(0, 1, k), xr)
            ship(("lp", k), w_at(0, 1, k), xl)
            share(0, 1, k)
        refresh(0, 1)
        for k in (1, 2):
            arrived(("r", k), w_at(3, 0, k), xl)
            if k == 1:
                ship(("rf", 0), w_at(3, 0, 1), xr)
            share(3, 0, k)
            arrived(("l", k), w_at(1, 0, k), xr)
            if k == 2:
                ship(("lf", 0), w_at(1, 0, 2), xl)
            share(1, 0, k)
        refresh(0, 2)
        arrived("rh", w_at(2, 0, 0).at[top], xl)
        arrived("lh", w_at(2, 0, 0).at[bottom], xr)
        ship(("ya", "F"), w_at(2, 0, 0), yp)
        share(2, 0, 0)
        arrived(("yo", 0), w_at(0, 1, 0), yp)
        share(0, 1, 0)
        for k in (1, 2):
            arrived(("rp", k), w_at(3, 1, k), xl)
            if k == 1:
                ship(("rf", 1), w_at(3, 1, 1), xr)
            share(3, 1, k)
            arrived(("lp", k), w_at(1, 1, k), xr)
            if k == 2:
                ship(("lf", 1), w_at(1, 1, 2), xl)
            share(1, 1, k)
        arrived(("ya", "L"), w_at(3, 1, 0), yp)
        share(3, 1, 0)
        arrived(("ya", "R"), w_at(1, 1, 0), yp)
        share(1, 1, 0)
        for dy in range(2):
            arrived(("rf", dy), w_at(2, dy, 1), xl)
            share(2, dy, 1)
            arrived(("lf", dy), w_at(2, dy, 2), xr)
            share(2, dy, 2)
        arrived(("ya", "F"), w_at(2, 1, 0), yp)
        share(2, 1, 0)
        for dx, dy, k in ORDER:
            arrived(("d", dx, dy, k), wg.at[slot(dx, dy, 1 - c, k)], sib)

    load_x[0].wait()
    transpose(xraw, 0, 0)
    arrived(("x", 0), xpeer.at[0], sib)
    transpose(xpeer, 0, 1)
    load_a.wait()
    gate(0, wait_weights)
    for k in range(OWN):
        wown[k] = wbuf[place[2, OWN * r + k]]

    def meanwhile():
        load_x[1].wait()
        transpose(xraw, 1, 0)
        arrived(("x", 1), xpeer.at[1], sib)
        transpose(xpeer, 1, 1)

    reduce_blocks(0, meanwhile)
    load_f.wait()
    load_q.wait()
    gather_blocks()

    def lay_out(j, carry):
        for i in range(RB):
            wbuf[j * RB + i] = wg[owner[0, i * CB + j]]
        return carry
    lax.fori_loop(0, CB, lay_out, 0)
    gate(1, None)
    reduce_blocks(1, lambda: None)
    for k in range(OWN):
        finish_sum(1, k)
        wout[0, k] = update(k)
    for k in range(OWN):
        refresh(1, k)
        for e in range(2):
            rout[0, k, e] = qbuf[k, e]
    for copy in started:
        copy.wait_send()


def body(features, grad_act, weights, owner_slot, factors, roots, helper_list):
    ids = jnp.arange(RB * CB, dtype=jnp.int32)
    rows, cols = ids // CB, ids % CB
    kinds = jnp.arange(3, dtype=jnp.int32)[:, None]
    wanted = jnp.where(kinds == 0, rows, jnp.where(kinds == 1, cols, cols * RB + rows))
    placing = owner_slot[0][None, :] == ids[:, None]
    place = jnp.sum(jnp.where(placing[None], wanted[:, None, :], 0), axis=2)
    listing = jnp.swapaxes(helper_list, 1, 2)
    tokens = features.shape[1]
    anywhere = pl.BlockSpec(memory_space=pl.ANY)
    scalars = pl.BlockSpec(memory_space=pltpu.SMEM)
    local = pl.BlockSpec(memory_space=pltpu.VMEM)
    block = (B, B)
    return pl.pallas_call(
        kernel,
        out_shape=(
            jax.ShapeDtypeStruct((1, OWN) + block, BF16),
            jax.ShapeDtypeStruct((1, OWN, 2) + block, BF16),
        ),
        in_specs=[scalars, scalars, local] + [anywhere] * 5,
        out_specs=(local, local),
        scratch_shapes=[
            pltpu.VMEM((2, tokens, RB * B), BF16),
            pltpu.VMEM((2, tokens, RB * B), BF16),
            pltpu.VMEM((RB, B, 2 * tokens), BF16),
            pltpu.VMEM((RB, B, 2 * tokens), BF16),
            pltpu.VMEM((CB * RB,) + block, BF16),
            pltpu.VMEM((2, tokens, CB * B), BF16),
            pltpu.VMEM((CB, 2 * tokens, B), BF16),
            pltpu.VMEM((CB, 2 * tokens, B), BF16),
            pltpu.VMEM((2, len(ORDER)) + block, BF16),
            pltpu.VMEM((RB * CB,) + block, BF16),
            pltpu.VMEM((OWN,) + block, BF16),
            pltpu.VMEM((OWN,) + block, F32),
            pltpu.VMEM((OWN, 2) + block, F32),
            pltpu.VMEM((OWN, 2) + block, BF16),
            pltpu.VMEM((2, 2, 2) + block, BF16),
            pltpu.VMEM((2, 2, 2) + block, BF16),
            pltpu.VMEM((2, 2, 2) + block, BF16),
            pltpu.VMEM((2, 4) + block, BF16),
            pltpu.VMEM((2, 2, H, B), BF16),
            pltpu.VMEM((2, 2, H, B), BF16),
            pltpu.VMEM((2, 2, H, B), BF16),
            pltpu.VMEM((2, 2) + block, BF16),
            pltpu.SemaphoreType.DMA((len(NAMES),)),
            pltpu.SemaphoreType.DMA((len(NAMES),)),
            pltpu.SemaphoreType.DMA((16,)),
        ],
        compiler_params=pltpu.CompilerParams(
            collective_id=0, has_side_effects=True, vmem_limit_bytes=60 * 1024 * 1024
        ),
    )(place, owner_slot, listing, features, grad_act, weights, factors, roots)


def solution(mesh):
    return jax.shard_map(
        body,
        mesh=mesh,
        in_specs=(
            P(None, "rep", None),
            P(None, "rep", "blk"),
            P(None, "blk"),
            P("blk", None),
            P("blk", "rep", None, None, None),
            P("blk", "rep", None, None, None),
            P(),
        ),
        out_specs=(P("blk", "rep", None, None), P("blk", "rep", None, None, None)),
        check_vma=False,
    )
```

time: 322 us -> 107 us (0.33)
  waiting for transfers between devices: 159 us -> 0 us
  Pallas kernels: 0 us -> 99.5 us
  matrix products: 71.7 us -> 0 us
  local copies, waits for them, and re-layouts: 65.5 us -> 3.83 us
  between operations: 14 us -> 0.66 us
  other arithmetic: 10.2 us -> 1.5 us
    reduce_scatter x2 -> x0, waiting for transfers between devices: 121 us -> none  [body(): lax.psum_scatter(jnp.einsum('tsa,tsb->sab', left_rows, right_cols, prefer...]
    pallas_call x0 -> x1, Pallas kernels: none -> 99.5 us  [body(): pl.pallas_call(kernel, out_shape=(jax.ShapeDtypeStruct((1, OWN) + block,...]
    dot_general x19 -> x0, matrix products: 71.7 us -> none  [the longest x12 29 us: exact_dot(): return jnp.einsum('...ij,...jk->...ik', first, second)]
    all_gather x1 -> x0, waiting for transfers between devices: 37.6 us -> none  [body(): lax.all_gather(own_weight, 'rep', axis=0, tiled=True)]
    gather x5 -> x0, local copies, waits for them, and re-layouts: 23 us -> none  [the longest x2 9.8 us: body(): left_rows = jnp.take(feature_blocks, block_at // col_blocks, axis=1)]
    reshape x3 -> x0, local copies, waits for them, and re-layouts: 22.7 us -> none  [the longest x2 21.3 us: body(): grid = weights.reshape(row_blocks, block_size, col_blocks, block_size)]
    transpose x1 -> x0, local copies, waits for them, and re-layouts: 8.92 us -> none  [body(): jnp.einsum('tsa,sab->tsb', chosen, lax.all_gather(own_weight, 'rep', axis...]
    reduce_sum x5 -> x1, other arithmetic: 4.36 us -> 0.73 us  [body(): place = jnp.sum(jnp.where(placing[None], wanted[:, None, :], 0), axis=2)]
  transfers between devices with their start and end apart: 3 -> 0, of which waited for: 3 -> 0; matrix products, arithmetic and copies ran while one was open for 11% -> 0% of each run, Pallas kernels for 0% -> 0%
where the time goes in v1:
time: 107 us; the launch traced here: 105 us
  Pallas kernels  99.5 us (93%)
  local copies, waits for them, and re-layouts  3.83 us (4%)
  other arithmetic  1.5 us (1%)
    pallas_call x1, Pallas kernels, body(): pl.pallas_call(kernel, out_shape=(jax.ShapeDtypeStruct((1, OWN) + block,...  99.5 us
    unnamed x2, local copies, waits for them, and re-layouts  3.83 us

profile of v1, /device:TPU:8, one launch (start us, length us, event | category | flops | bytes accessed | tf_op | source)
XLA Modules:
  0.0 105.5 jit_solution(1707656988743102584)
XLA Ops:
  0.7 0.1 select_select_fusion
  0.7 0.7 iota_compare_fusion
  1.4 0.7 select_reduce_fusion.place
  2.1 99.5 %shard_map.89 = (bf16[1,3,256,256]{3,2,1,0:T(8,128)(2,1)}, bf16[1,3,2,256,256]{4,3,2,1,0:T(8,128)(2,1)}) custom-call(s32[3,48]{1,0:T(4,128)} %select_reduce_fusion.place, s32[1,48]{1,0:T(1,128)} %owner.1, s32[2,4,16]{2,1,0:T(4,128)} %bitcast.2, bf16[2,256,2048]{2,1,0:T(8,128)(2,1)} %feat.1, bf16[2,256,1536]{2,1,0:T(8,128)(2,1)} %act.1, ...), custom_call_target="tpu_custom_call" | custom-call | tf_op jit(solution)/shard_map/pallas_call | solution.py:420
  101.6 1.8 %copy.11 = bf16[1,3,256,256]{3,2,1,0:T(8,128)(2,1)} copy(bf16[1,3,256,256]{3,2,1,0:T(8,128)(2,1)} %get-tuple-element.8) | data formatting | bytes 786432
  103.4 2.1 %copy.12 = bf16[1,3,2,256,256]{4,3,2,1,0:T(8,128)(2,1)} copy(bf16[1,3,2,256,256]{4,3,2,1,0:T(8,128)(2,1)} %get-tuple-element.9) | data formatting | bytes 1572864
  (3 shorter events, 0.0 us)

commit v2 on v1

--- a/solution.py
+++ b/solution.py
@@ -22,10 +22,10 @@
 MESH = pl.DeviceIdType.MESH
 
 ORDER = (
-    [(2, 1, 1), (2, 1, 2), (2, 0, 1), (2, 0, 2)]
-    + [(2, 1, 0), (1, 1, 0), (3, 1, 0), (0, 1, 0)]
-    + [(1, 1, 2), (3, 1, 1), (1, 0, 2), (3, 0, 1)]
-    + [(1, 1, 1), (3, 1, 2), (1, 0, 1), (3, 0, 2)]
+    [(2, 1, 1), (2, 1, 2), (2, 1, 0), (2, 0, 1), (2, 0, 2)]
+    + [(1, 1, 0), (3, 1, 0), (0, 1, 0)]
+    + [(1, 1, 2), (3, 1, 1), (1, 1, 1), (3, 1, 2)]
+    + [(1, 0, 2), (3, 0, 1), (1, 0, 1), (3, 0, 2)]
     + [(2, 0, 0), (1, 0, 0), (3, 0, 0), (0, 0, 0)]
     + [(0, 1, 1), (0, 1, 2), (0, 0, 1), (0, 0, 2)]
 )
@@ -146,11 +146,12 @@
             return carry
         lax.fori_loop(0, RB, turn, 0)
 
-    def gate(t, ready):
+    def gate(t, ready, block):
         def one(j, carry):
-            if ready is not None:
-                ready(j)
-            value = dot(xraw[t], wbuf[pl.ds(j * RB, RB)].reshape(RB * B, B))
+            ready(j)
+            value = dot(xraw[t, :, 0:B], block(0, j))
+            for i in range(1, RB):
+                value = value + dot(xraw[t, :, i * B:(i + 1) * B], block(i, j))
             sigmoid = 1.0 / (1.0 + jnp.exp(-value))
             slope = sigmoid * (1.0 + value * (1.0 - sigmoid))
             cols = pl.ds(pl.multiple_of(j * B, B), B)
@@ -160,44 +161,52 @@
             ).start()
             return carry
         lax.fori_loop(0, CB, one, 0)
+
+    def wait_dgate(t):
         for j in range(CB):
             own = db[t].at[j, pl.ds(0, B), :]
             other = db[t].at[j, pl.ds(B, B), :]
             started.append(remote(NAMES[("D", t, j)], own, other, sib))
             arrived(("D", t, j), other, sib)
 
-    def partials(t, first, count):
+    def partial(t, at, here):
+        pb[t, at] = low(dot(xt[t][place[0, here]], db[t][place[1, here]]))
+
+    def partials(t, first, count, looped=False):
         slots = [slot(dx, dy, c, k) for dx, dy, k in ORDER[first:first + count]]
+        if not looped:
+            for m in range(count):
+                partial(t, first + m, slots[m])
+            return
 
         def one(n, carry):
             here = slots[0]
             for m in range(1, count):
                 here = jnp.where(n == m, slots[m], here)
-            pb[t, first + n] = low(dot(xt[t][place[0, here]], db[t][place[1, here]]))
+            partial(t, first + n, here)
             return carry
         lax.fori_loop(0, count, one, 0)
 
     def p(t, dx, dy, k):
         return pb.at[t, PLACE[(dx, dy, k)]]
 
+    side = ((xr, 1, xl), (xl, 3, xr))
+    land = (froml, fromr)
+    halves = (pl.ds(0, H), pl.ds(H, H))
+    land_a = (fromla, fromra)
+
     def reduce_blocks(t, between):
-        side = ((xr, 1, xl), (xl, 3, xr))
-        partials(t, 0, 4)
-        for dy in (1, 0):
+        def start(dy):
             for way in range(2):
                 send(("s1", t, way, dy), p(t, 2, dy, 1 + way), fwdb.at[t, way, dy], side[way][0])
-        partials(t, 4, 4)
-        for dx in (2, 1, 3, 0):
-            send(("a1", t, dx), p(t, dx, 1, 0), ya.at[t, dx], yp)
-        partials(t, 8, 4)
-        land = (froml, fromr)
-        for dy in (1, 0):
+
+        def near(dy):
             for way in range(2):
                 k = 2 - way
                 send(("in", t, way, dy), p(t, side[way][1], dy, k), land[way].at[t, dy, k - 1], side[way][0])
-        for first in (12, 16, 20):
-            partials(t, first, 4)
-        between()
+
+        def across(dx):
+            send(("a1", t, dx), p(t, dx, 1, 0), ya.at[t, dx], yp)
 
         def pass_on(dy):
             for way in range(2):
@@ -211,49 +220,61 @@
             arrived(("a1", t, dx), ya.at[t, dx], yp)
             return p(t, dx, 0, 0)[...].astype(F32) + ya[t, dx].astype(F32)
 
-        halves = (pl.ds(0, H), pl.ds(H, H))
-        land_a = (fromla, fromra)
+        partials(t, 0, 2)
+        start(1)
+        partials(t, 2, 1)
+        across(2)
+        partials(t, 3, 2)
+        start(0)
+        partials(t, 5, 3)
+        for dx in (1, 3, 0):
+            across(dx)
+        partials(t, 8, 4)
+        near(1)
+        for first in (12, 16, 20):
+            partials(t, first, 4, looped=True)
+        between()
         pass_on(1)
         p(t, 2, 0, 0)[...] = low(add_y(2))
         for way in range(2):
             send(("fa", t, way), p(t, 2, 0, 0).at[halves[way]], fwda.at[t, way], side[way][0])
+        near(0)
         pass_on(0)
         for way in range(2):
             dx = side[way][1]
             p(t, dx, 0, 0)[...] = low(add_y(dx))
             send(("ia", t, way), p(t, dx, 0, 0).at[halves[1 - way]], land_a[way].at[t, 1 - way], side[way][0])
         gbuf[0] = add_y(0)
+        for k in (1, 2):
+            p(t, 0, 1, k)[...] = low(summed(t, 1, k))
+            send(("b2", t, k), p(t, 0, 1, k), yb.at[t, k - 1], yp)
         for way in range(2):
             arrived(("fa", t, way), fwda.at[t, way], side[way][2])
             mine = p(t, side[way][1], 0, 0).at[halves[way]]
             mine[...] = low(mine[...].astype(F32) + fwda[t, way].astype(F32))
             send(("da", t, way), mine, land_a[way].at[t, way], side[way][0])
 
-        def summed(dy, k):
-            for way in range(2):
-                kind = "de" if k == 1 + way else "in"
-                arrived((kind, t, way, dy), land[way].at[t, dy, k - 1], side[way][2])
-            return (
-                p(t, 0, dy, k)[...].astype(F32)
-                + froml[t, dy, k - 1].astype(F32) + fromr[t, dy, k - 1].astype(F32)
-            )
-
-        for k in (1, 2):
-            p(t, 0, 1, k)[...] = low(summed(1, k))
-            send(("b2", t, k), p(t, 0, 1, k), yb.at[t, k - 1], yp)
-        for k in (1, 2):
-            gbuf[k] = summed(0, k)
+    def summed(t, dy, k):
+        for way in range(2):
+            kind = "de" if k == 1 + way else "in"
+            arrived((kind, t, way, dy), land[way].at[t, dy, k - 1], side[way][2])
+        return (
+            p(t, 0, dy, k)[...].astype(F32)
+            + froml[t, dy, k - 1].astype(F32) + fromr[t, dy, k - 1].astype(F32)
+        )
+
+    def finish_sum(t, k):
+        if k > 0:
+            value = summed(t, 0, k)
+            arrived(("b2", t, k), yb.at[t, k - 1], yp)
+            gbuf[k] = value + yb[t, k - 1].astype(F32)
+            return
         for way in range(2):
             arrived(("ia", t, way), land_a[way].at[t, 1 - way], side[way][2])
             arrived(("da", t, way), land_a[way].at[t, way], side[way][2])
         for half in range(2):
             rows = slice(half * H, (half + 1) * H)
             gbuf[0, rows, :] += fromla[t, half].astype(F32) + fromra[t, half].astype(F32)
-
-    def finish_sum(t, k):
-        if k > 0:
-            arrived(("b2", t, k), yb.at[t, k - 1], yp)
-            gbuf[k] = gbuf[k] + yb[t, k - 1].astype(F32)
 
     def update(k):
         grad = gbuf[k]
@@ -265,31 +286,38 @@
         wown[k] = value
         return value
 
-    def refresh(t, k):
-        grad = low(gbuf[k])
-        turned = grad.T
+    def refresh(t, owned):
         rows = lax.broadcasted_iota(jnp.int32, (B, B), 0)
         cols = lax.broadcasted_iota(jnp.int32, (B, B), 1)
         diagonal = rows == cols
         five = jnp.where(diagonal, F32(5.0), F32(0.0))
-        stats = (dot(grad, turned), dot(turned, grad))
-        for e in range(2):
-            fresh = DECAY * fbuf[k, e] + (1.0 - DECAY) * stats[e]
+        ridge = jnp.where(diagonal, F32(RIDGE), F32(0.0))
+        sides = [(k, e) for k in owned for e in range(2)]
+        stats = []
+        for k in owned:
+            grad = low(gbuf[k])
+            turned = grad.T
+            stats += [dot(grad, turned), dot(turned, grad)]
+        current, factor, result = [], [], []
+        for (k, e), stat in zip(sides, stats):
+            fresh = DECAY * fbuf[k, e] + (1.0 - DECAY) * stat
             fbuf[k, e] = fresh
-            ridged = fresh + jnp.where(diagonal, F32(RIDGE), F32(0.0))
+            ridged = fresh + ridge
             scale = jnp.sqrt(total(ridged * ridged) + NORM_EPS)
-            current = ridged / scale
-            factor = (five - current) * 0.25
-            result = factor / jnp.sqrt(jnp.sqrt(scale))
-            for turn in range(1, NEWTON):
-                factor_low = low(factor)
-                square = low(dot(factor_low, factor_low))
-                current = dot(low(dot(square, square)), low(current))
-                factor = (five - current) * 0.25
-                result = dot(low(result), low(factor))
+            current.append(ridged / scale)
+            factor.append((five - current[-1]) * 0.25)
+            result.append(low(factor[-1] / jnp.sqrt(jnp.sqrt(scale))))
+        for turn in range(1, NEWTON):
+            factor = [low(value) for value in factor]
+            square = [low(dot(value, value)) for value in factor]
+            fourth = [low(dot(value, value)) for value in square]
+            current = [dot(value, low(old)) for value, old in zip(fourth, current)]
+            factor = [(five - value) * 0.25 for value in current]
+            result = [low(dot(old, low(value))) for old, value in zip(result, factor)]
+        for (k, e), value in zip(sides, result):
             name = group * (2 * OWN) + 2 * k + e
             hits = total(jnp.where(listing[t] == name, F32(1.0), F32(0.0)))
-            qbuf[k, e] = jnp.where(hits > 0.5, low(result), qbuf[k, e])
+            qbuf[k, e] = jnp.where(hits > 0.5, value, qbuf[k, e])
 
     def w_at(dx, dy, k):
         return wg.at[slot(dx, dy, c, k)]
@@ -302,17 +330,29 @@
         def ship(name, ref, dev):
             send(name, ref, ref, dev)
 
-        for k in range(OWN):
+        for k in (1, 2, 0):
             finish_sum(0, k)
             wg[slot(0, 0, c, k)] = update(k)
+            ship(("yo", k), w_at(0, 0, k), yp)
             ship(("r", k), w_at(0, 0, k), xr)
             ship(("l", k), w_at(0, 0, k), xl)
-            if k > 0:
-                ship(("yo", k), w_at(0, 0, k), yp)
             share(0, 0, k)
-        ship(("yo", 0), w_at(0, 0, 0), yp)
-        refresh(0, 0)
         top, bottom = pl.ds(0, H), pl.ds(H, H)
+        refresh(0, (1,))
+        arrived(("r", 1), w_at(3, 0, 1), xl)
+        share(3, 0, 1)
+        arrived(("l", 1), w_at(1, 0, 1), xr)
+        share(1, 0, 1)
+        refresh(0, (2,))
+        for k in (1, 2):
+            arrived(("yo", k), w_at(0, 1, k), yp)
+            ship(("rp", k), w_at(0, 1, k), xr)
+            ship(("lp", k), w_at(0, 1, k), xl)
+            share(0, 1, k)
+        arrived(("r", 2), w_at(3, 0, 2), xl)
+        share(3, 0, 2)
+        arrived(("l", 2), w_at(1, 0, 2), xr)
+        share(1, 0, 2)
         arrived(("r", 0), w_at(3, 0, 0), xl)
         ship("rh", w_at(3, 0, 0).at[top], xr)
         ship(("ya", "L"), w_at(3, 0, 0), yp)
@@ -321,26 +361,9 @@
         ship("lh", w_at(1, 0, 0).at[bottom], xl)
         ship(("ya", "R"), w_at(1, 0, 0), yp)
         share(1, 0, 0)
-        for k in (1, 2):
-            arrived(("yo", k), w_at(0, 1, k), yp)
-            ship(("rp", k), w_at(0, 1, k), xr)
-            ship(("lp", k), w_at(0, 1, k), xl)
-            share(0, 1, k)
-        refresh(0, 1)
-        for k in (1, 2):
-            arrived(("r", k), w_at(3, 0, k), xl)
-            if k == 1:
-                ship(("rf", 0), w_at(3, 0, 1), xr)
-            share(3, 0, k)
-            arrived(("l", k), w_at(1, 0, k), xr)
-            if k == 2:
-                ship(("lf", 0), w_at(1, 0, 2), xl)
-            share(1, 0, k)
-        refresh(0, 2)
-        arrived("rh", w_at(2, 0, 0).at[top], xl)
-        arrived("lh", w_at(2, 0, 0).at[bottom], xr)
-        ship(("ya", "F"), w_at(2, 0, 0), yp)
-        share(2, 0, 0)
+        ship(("rf", 0), w_at(3, 0, 1), xr)
+        ship(("lf", 0), w_at(1, 0, 2), xl)
+        refresh(0, (0,))
         arrived(("yo", 0), w_at(0, 1, 0), yp)
         share(0, 1, 0)
         for k in (1, 2):
@@ -354,6 +377,10 @@
             share(1, 1, k)
         arrived(("ya", "L"), w_at(3, 1, 0), yp)
         share(3, 1, 0)
+        arrived("rh", w_at(2, 0, 0).at[top], xl)
+        arrived("lh", w_at(2, 0, 0).at[bottom], xr)
+        ship(("ya", "F"), w_at(2, 0, 0), yp)
+        share(2, 0, 0)
         arrived(("ya", "R"), w_at(1, 1, 0), yp)
         share(1, 1, 0)
         for dy in range(2):
@@ -368,40 +395,53 @@
 
     load_x[0].wait()
     transpose(xraw, 0, 0)
+    load_a.wait()
+    gate(0, wait_weights, lambda i, j: wbuf[j * RB + i])
     arrived(("x", 0), xpeer.at[0], sib)
     transpose(xpeer, 0, 1)
-    load_a.wait()
-    gate(0, wait_weights)
-    for k in range(OWN):
-        wown[k] = wbuf[place[2, OWN * r + k]]
+    wait_dgate(0)
 
     def meanwhile():
+        for k in range(OWN):
+            wown[k] = wbuf[place[2, OWN * r + k]]
         load_x[1].wait()
         transpose(xraw, 1, 0)
         arrived(("x", 1), xpeer.at[1], sib)
         transpose(xpeer, 1, 1)
+        load_f.wait()
+        load_q.wait()
 
     reduce_blocks(0, meanwhile)
-    load_f.wait()
-    load_q.wait()
     gather_blocks()
 
-    def lay_out(j, carry):
-        for i in range(RB):
-            wbuf[j * RB + i] = wg[owner[0, i * CB + j]]
-        return carry
-    lax.fori_loop(0, CB, lay_out, 0)
-    gate(1, None)
+    gate(1, lambda j: None, lambda i, j: wg[owner[0, i * CB + j]])
+    wait_dgate(1)
     reduce_blocks(1, lambda: None)
-    for k in range(OWN):
-        finish_sum(1, k)
-        wout[0, k] = update(k)
-    for k in range(OWN):
-        refresh(1, k)
-        for e in range(2):
-            rout[0, k, e] = qbuf[k, e]
+    for ks in ((1, 2), (0,)):
+        for k in ks:
+            finish_sum(1, k)
+            wout[0, k] = update(k)
+        refresh(1, ks)
+        for k in ks:
+            for e in range(2):
+                rout[0, k, e] = qbuf[k, e]
     for copy in started:
         copy.wait_send()
+
+
+def deliver(weights, roots, wout, rout, held, insem, outsem):
+    pieces = [(weights.at[0, k], wout.at[0, k]) for k in range(OWN)]
+    pieces += [(roots.at[0, k, e], rout.at[0, k, e]) for k in range(OWN) for e in range(2)]
+    incoming, outgoing = [], []
+    for n, (src, dst) in enumerate(pieces):
+        incoming.append(pltpu.make_async_copy(src, held.at[n], insem.at[n]))
+        outgoing.append(pltpu.make_async_copy(held.at[n], dst, outsem.at[n]))
+        incoming[n].start()
+    for n in range(len(pieces)):
+        incoming[n].wait()
+        outgoing[n].start()
+    for n in range(len(pieces)):
+        outgoing[n].wait()
 
 
 def body(features, grad_act, weights, owner_slot, factors, roots, helper_list):
@@ -417,12 +457,13 @@
     scalars = pl.BlockSpec(memory_space=pltpu.SMEM)
     local = pl.BlockSpec(memory_space=pltpu.VMEM)
     block = (B, B)
-    return pl.pallas_call(
+    results = (
+        jax.ShapeDtypeStruct((1, OWN) + block, BF16),
+        jax.ShapeDtypeStruct((1, OWN, 2) + block, BF16),
+    )
+    made = pl.pallas_call(
         kernel,
-        out_shape=(
-            jax.ShapeDtypeStruct((1, OWN) + block, BF16),
-            jax.ShapeDtypeStruct((1, OWN, 2) + block, BF16),
-        ),
+        out_shape=results,
         in_specs=[scalars, scalars, local] + [anywhere] * 5,
         out_specs=(local, local),
         scratch_shapes=[
@@ -456,6 +497,17 @@
             collective_id=0, has_side_effects=True, vmem_limit_bytes=60 * 1024 * 1024
         ),
     )(place, owner_slot, listing, features, grad_act, weights, factors, roots)
+    return pl.pallas_call(
+        deliver,
+        out_shape=results,
+        in_specs=[anywhere] * 2,
+        out_specs=(anywhere, anywhere),
+        scratch_shapes=[
+            pltpu.VMEM((3 * OWN,) + block, BF16),
+            pltpu.SemaphoreType.DMA((3 * OWN,)),
+            pltpu.SemaphoreType.DMA((3 * OWN,)),
+        ],
+    )(*made)
 
 
 def solution(mesh):

time: 107 us -> 94.9 us (0.89); the launches traced: 105 us -> 94.7 us
  Pallas kernels: 99.5 us -> 92.4 us
  local copies, waits for them, and re-layouts: 3.83 us -> 0 us
    pallas_call x1 -> x2, Pallas kernels: 99.5 us -> 92.4 us  [the longest x1 90.2 us: body(): pl.pallas_call(kernel, out_shape=results, in_specs=[scalars, scalars, loc...]
    unnamed x2 -> x0, local copies, waits for them, and re-layouts: 3.83 us -> none
where the time goes in v2:
time: 94.9 us; the launch traced here: 94.7 us
  Pallas kernels  92.4 us (97%)
  other arithmetic  1.5 us (2%)
    pallas_call x1, Pallas kernels, body(): pl.pallas_call(kernel, out_shape=results, in_specs=[scalars, scalars, loc...  90.2 us
    pallas_call x1, Pallas kernels, body(): pl.pallas_call(deliver, out_shape=results, in_specs=[anywhere] * 2, out_s...  2.15 us

profile of v2, /device:TPU:8, one launch (start us, length us, event | category | flops | bytes accessed | tf_op | source)
XLA Modules:
  0.0 94.7 jit_solution(5784924801599476158)
XLA Ops:
  0.7 0.1 select_select_fusion
  0.7 0.7 iota_compare_fusion
  1.4 0.7 select_reduce_fusion.place
  2.1 90.2 %shard_map.89 = (bf16[1,3,256,256]{3,2,1,0:T(8,128)(2,1)}, bf16[1,3,2,256,256]{4,3,2,1,0:T(8,128)(2,1)}) custom-call(s32[3,48]{1,0:T(4,128)} %select_reduce_fusion.place, s32[1,48]{1,0:T(1,128)} %owner.1, s32[2,4,16]{2,1,0:T(4,128)} %bitcast.2, bf16[2,256,2048]{2,1,0:T(8,128)(2,1)} %feat.1, bf16[2,256,1536]{2,1,0:T(8,128)(2,1)} %act.1, ...), custom_call_target="tpu_custom_call" | custom-call | tf_op jit(solution)/shard_map/pallas_call | solution.py:464
  92.4 2.1 %shard_map.90 = (bf16[1,3,256,256]{3,2,1,0:T(8,128)(2,1)}, bf16[1,3,2,256,256]{4,3,2,1,0:T(8,128)(2,1)}) custom-call(bf16[1,3,256,256]{3,2,1,0:T(8,128)(2,1)} %get-tuple-element.4.weights, bf16[1,3,2,256,256]{4,3,2,1,0:T(8,128)(2,1)} %get-tuple-element.5.roots), custom_call_target="tpu_custom_call" | custom-call | tf_op jit(solution)/shard_map/pallas_call | solution.py:500
  (3 shorter events, 0.0 us)

commit v3 on v2

--- a/solution.py
+++ b/solution.py
@@ -69,11 +69,11 @@
 def kernel(
     place, owner, listing, feat, act, wts, fac, rts,
     wout, rout,
-    xraw, xpeer, xt0, xt1, wbuf, actb, db0, db1, pb, wg, wown, gbuf, fbuf, qbuf,
+    xraw, xpeer, xt0, xt1, wbuf, actb, own0, own1, other0, other1, pb, wg, wown, gbuf, fbuf, qbuf,
     fwdb, froml, fromr, ya, fwda, fromla, fromra, yb,
     ssem, rsem, lsem,
 ):
-    xt, db = (xt0, xt1), (db0, db1)
+    xt, db = (xt0, xt1), ((own0, other0), (own1, other1))
     r = lax.axis_index("rep")
     group = lax.axis_index("blk")
     c = lax.rem(r, 2)
@@ -107,11 +107,12 @@
         pltpu.make_async_copy(columns, columns, lsem.at[j]).wait()
 
     load_x = [load(CB, feat.at[0], xraw.at[0])]
+    load_a = load(CB + 1, act.at[0], actb.at[0])
     for j in range(CB):
         for i in range(RB):
             load(j, wts.at[pl.ds(i * B, B), pl.ds(j * B, B)], wbuf.at[j * RB + i])
-    load_a = load(CB + 1, act, actb)
     load_x.append(load(CB + 2, feat.at[1], xraw.at[1]))
+    load_b = load(CB + 5, act.at[1], actb.at[1])
     load_f = load(CB + 3, fac.at[0], fbuf)
     load_q = load(CB + 4, rts.at[0], qbuf)
 
@@ -139,38 +140,54 @@
     for t in range(2):
         send(("x", t), feat.at[t], xpeer.at[t], sib)
 
+    def turn(src, t, half, i):
+        cols = pl.ds(pl.multiple_of(i * B, B), B)
+        xt[t][i, :, half * B:(half + 1) * B] = src[t, :, cols].T
+
     def transpose(src, t, half):
-        def turn(i, carry):
-            cols = pl.ds(pl.multiple_of(i * B, B), B)
-            xt[t][i, :, half * B:(half + 1) * B] = src[t, :, cols].T
+        def one(i, carry):
+            turn(src, t, half, i)
             return carry
-        lax.fori_loop(0, RB, turn, 0)
-
-    def gate(t, ready, block):
-        def one(j, carry):
-            ready(j)
-            value = dot(xraw[t, :, 0:B], block(0, j))
-            for i in range(1, RB):
-                value = value + dot(xraw[t, :, i * B:(i + 1) * B], block(i, j))
-            sigmoid = 1.0 / (1.0 + jnp.exp(-value))
-            slope = sigmoid * (1.0 + value * (1.0 - sigmoid))
-            cols = pl.ds(pl.multiple_of(j * B, B), B)
-            db[t][j, 0:B, :] = low(actb[t, :, cols].astype(F32) * slope)
-            remote(
-                NAMES[("D", t, 0)] + j, db[t].at[j, pl.ds(0, B), :], db[t].at[j, pl.ds(B, B), :], sib
-            ).start()
+        lax.fori_loop(0, RB, one, 0)
+
+    def gate(t, ready, block, beside):
+        def pair(n, carry):
+            columns = (2 * n, 2 * n + 1)
+            values = []
+            for j in columns:
+                ready(j)
+            for j in columns:
+                value = dot(xraw[t, :, 0:B], block(0, j))
+                for i in range(1, RB):
+                    value = value + dot(xraw[t, :, i * B:(i + 1) * B], block(i, j))
+                values.append(value)
+            beside(n)
+            for j, value in zip(columns, values):
+                sigmoid = 1.0 / (1.0 + jnp.exp(-value))
+                slope = sigmoid * (1.0 + value * (1.0 - sigmoid))
+                cols = pl.ds(pl.multiple_of(j * B, B), B)
+                db[t][0][j] = low(actb[t, :, cols].astype(F32) * slope)
+            for j in columns:
+                remote(
+                    NAMES[("D", t, 0)] + j, db[t][0].at[j], db[t][1].at[j], sib
+                ).start()
             return carry
-        lax.fori_loop(0, CB, one, 0)
+        lax.fori_loop(0, CB // 2, pair, 0)
+        for m, (dx, dy, k) in enumerate(ORDER[:2]):
+            gbuf[1 + m] = half_product(t, slot(dx, dy, c, k), 0)
+
+    def half_product(t, here, half):
+        part = slice(half * B, (half + 1) * B)
+        return dot(xt[t][place[0, here], :, part], db[t][half][place[1, here]])
 
     def wait_dgate(t):
         for j in range(CB):
-            own = db[t].at[j, pl.ds(0, B), :]
-            other = db[t].at[j, pl.ds(B, B), :]
+            own, other = db[t][0].at[j], db[t][1].at[j]
             started.append(remote(NAMES[("D", t, j)], own, other, sib))
             arrived(("D", t, j), other, sib)
 
     def partial(t, at, here):
-        pb[t, at] = low(dot(xt[t][place[0, here]], db[t][place[1, here]]))
+        pb[t, at] = low(half_product(t, here, 0) + half_product(t, here, 1))
 
     def partials(t, first, count, looped=False):
         slots = [slot(dx, dy, c, k) for dx, dy, k in ORDER[first:first + count]]
@@ -220,7 +237,8 @@
             arrived(("a1", t, dx), ya.at[t, dx], yp)
             return p(t, dx, 0, 0)[...].astype(F32) + ya[t, dx].astype(F32)
 
-        partials(t, 0, 2)
+        for m, (dx, dy, k) in enumerate(ORDER[:2]):
+            pb[t, m] = low(gbuf[1 + m] + half_product(t, slot(dx, dy, c, k), 1))
         start(1)
         partials(t, 2, 1)
         across(2)
@@ -394,9 +412,13 @@
             arrived(("d", dx, dy, k), wg.at[slot(dx, dy, 1 - c, k)], sib)
 
     load_x[0].wait()
-    transpose(xraw, 0, 0)
     load_a.wait()
-    gate(0, wait_weights, lambda i, j: wbuf[j * RB + i])
+
+    def turn_own(n):
+        for m in range(3):
+            turn(xraw, 0, 0, jnp.minimum(3 * n + m, RB - 1))
+
+    gate(0, wait_weights, lambda i, j: wbuf[j * RB + i], turn_own)
     arrived(("x", 0), xpeer.at[0], sib)
     transpose(xpeer, 0, 1)
     wait_dgate(0)
@@ -408,13 +430,14 @@
         transpose(xraw, 1, 0)
         arrived(("x", 1), xpeer.at[1], sib)
         transpose(xpeer, 1, 1)
+        load_b.wait()
         load_f.wait()
         load_q.wait()
 
     reduce_blocks(0, meanwhile)
     gather_blocks()
 
-    gate(1, lambda j: None, lambda i, j: wg[owner[0, i * CB + j]])
+    gate(1, lambda j: None, lambda i, j: wg[owner[0, i * CB + j]], lambda n: None)
     wait_dgate(1)
     reduce_blocks(1, lambda: None)
     for ks in ((1, 2), (0,)):
@@ -473,8 +496,10 @@
             pltpu.VMEM((RB, B, 2 * tokens), BF16),
             pltpu.VMEM((CB * RB,) + block, BF16),
             pltpu.VMEM((2, tokens, CB * B), BF16),
-            pltpu.VMEM((CB, 2 * tokens, B), BF16),
-            pltpu.VMEM((CB, 2 * tokens, B), BF16),
+            pltpu.VMEM((CB, tokens, B), BF16),
+            pltpu.VMEM((CB, tokens, B), BF16),
+            pltpu.VMEM((CB, tokens, B), BF16),
+            pltpu.VMEM((CB, tokens, B), BF16),
             pltpu.VMEM((2, len(ORDER)) + block, BF16),
             pltpu.VMEM((RB * CB,) + block, BF16),
             pltpu.VMEM((OWN,) + block, BF16),

time: 94.9 us -> 93.7 us (0.987)
  Pallas kernels: 92.4 us -> 90.6 us
    pallas_call x1, Pallas kernels: 90.2 us -> 88.5 us  [body(): pl.pallas_call(kernel, out_shape=results, in_specs=[scalars, scalars, loc...]
where the time goes in v3:
time: 93.7 us; the launch traced here: 93 us
  Pallas kernels  90.6 us (97%)
  other arithmetic  1.5 us (2%)
    pallas_call x1, Pallas kernels, body(): pl.pallas_call(kernel, out_shape=results, in_specs=[scalars, scalars, loc...  88.5 us
    pallas_call x1, Pallas kernels, body(): pl.pallas_call(deliver, out_shape=results, in_specs=[anywhere] * 2, out_s...  2.15 us

profile of v3, /device:TPU:8, one launch (start us, length us, event | category | flops | bytes accessed | tf_op | source)
XLA Modules:
  0.0 93.0 jit_solution(10389862438914480510)
XLA Ops:
  0.7 0.1 select_select_fusion
  0.7 0.7 iota_compare_fusion
  1.4 0.7 select_reduce_fusion.place
  2.1 88.5 %shard_map.89 = (bf16[1,3,256,256]{3,2,1,0:T(8,128)(2,1)}, bf16[1,3,2,256,256]{4,3,2,1,0:T(8,128)(2,1)}) custom-call(s32[3,48]{1,0:T(4,128)} %select_reduce_fusion.place, s32[1,48]{1,0:T(1,128)} %owner.1, s32[2,4,16]{2,1,0:T(4,128)} %bitcast.2, bf16[2,256,2048]{2,1,0:T(8,128)(2,1)} %feat.1, bf16[2,256,1536]{2,1,0:T(8,128)(2,1)} %act.1, ...), custom_call_target="tpu_custom_call" | custom-call | tf_op jit(solution)/shard_map/pallas_call | solution.py:487
  90.6 2.1 %shard_map.90 = (bf16[1,3,256,256]{3,2,1,0:T(8,128)(2,1)}, bf16[1,3,2,256,256]{4,3,2,1,0:T(8,128)(2,1)}) custom-call(bf16[1,3,256,256]{3,2,1,0:T(8,128)(2,1)} %get-tuple-element.4.weights, bf16[1,3,2,256,256]{4,3,2,1,0:T(8,128)(2,1)} %get-tuple-element.5.roots), custom_call_target="tpu_custom_call" | custom-call | tf_op jit(solution)/shard_map/pallas_call | solution.py:525
  (3 shorter events, 0.0 us)

commit v4 on v3

--- a/solution.py
+++ b/solution.py
@@ -12,7 +12,10 @@
 STEP_SIZE = 0.5
 
 B = 256
-H = B // 2
+S = 80
+RA = B + S
+R0 = 240
+PIECES = {"0": (0, 0, B), "1a": (1, 0, S), "1b": (1, S, B - S), "2": (2, 0, B)}
 OWN = 3
 RB = 8
 CB = 6
@@ -23,11 +26,11 @@
 
 ORDER = (
     [(2, 1, 1), (2, 1, 2), (2, 1, 0), (2, 0, 1), (2, 0, 2)]
-    + [(1, 1, 0), (3, 1, 0), (0, 1, 0)]
-    + [(1, 1, 2), (3, 1, 1), (1, 1, 1), (3, 1, 2)]
+    + [(1, 1, 0), (1, 1, 1), (3, 1, 0), (3, 1, 1), (1, 1, 2)]
+    + [(0, 1, 0), (0, 1, 1), (3, 1, 2)]
     + [(1, 0, 2), (3, 0, 1), (1, 0, 1), (3, 0, 2)]
     + [(2, 0, 0), (1, 0, 0), (3, 0, 0), (0, 0, 0)]
-    + [(0, 1, 1), (0, 1, 2), (0, 0, 1), (0, 0, 2)]
+    + [(0, 1, 2), (0, 0, 1), (0, 0, 2)]
 )
 PLACE = {item: q for q, item in enumerate(ORDER)}
 
@@ -42,12 +45,12 @@
         names += [("de", t, way, dy) for way in range(2) for dy in range(2)]
         names += [(kind, t, way) for kind in ("fa", "ia", "da") for way in range(2)]
         names += [("b2", t, k) for k in (1, 2)]
-    names += [(kind, k) for kind in ("yo", "r", "l") for k in range(OWN)]
-    names += [(kind, k) for kind in ("rp", "lp") for k in (1, 2)]
-    names += [("ya", place) for place in "LRF"]
-    names += ["rh", "lh"]
+    names += [(kind, piece) for kind in ("yo", "r", "l") for piece in PIECES]
+    names += [(kind, piece) for kind in ("rp", "lp") for piece in ("2", "1b")]
+    names += [("ya", place, piece) for place in "LRF" for piece in ("0", "1a")]
+    names += ["rh", "lh0", "lh1"]
     names += [(kind, dy) for kind in ("rf", "lf") for dy in range(2)]
-    names += [("d",) + item for item in ORDER]
+    names += [("d", dx, dy, piece) for dx in range(XN) for dy in range(2) for piece in PIECES]
     return {name: n for n, name in enumerate(names)}
 
 
@@ -69,7 +72,7 @@
 def kernel(
     place, owner, listing, feat, act, wts, fac, rts,
     wout, rout,
-    xraw, xpeer, xt0, xt1, wbuf, actb, own0, own1, other0, other1, pb, wg, wown, gbuf, fbuf, qbuf,
+    xraw, xpeer, xt0, xt1, wbuf, actb, own0, own1, other0, other1, pa, pb, wg, wown, ga, gbuf, fbuf, qbuf,
     fwdb, froml, fromr, ya, fwda, fromla, fromra, yb,
     ssem, rsem, lsem,
 ):
@@ -186,113 +189,129 @@
             started.append(remote(NAMES[("D", t, j)], own, other, sib))
             arrived(("D", t, j), other, sib)
 
-    def partial(t, at, here):
-        pb[t, at] = low(half_product(t, here, 0) + half_product(t, here, 1))
-
-    def partials(t, first, count, looped=False):
-        slots = [slot(dx, dy, c, k) for dx, dy, k in ORDER[first:first + count]]
-        if not looped:
-            for m in range(count):
-                partial(t, first + m, slots[m])
-            return
-
-        def one(n, carry):
-            here = slots[0]
-            for m in range(1, count):
-                here = jnp.where(n == m, slots[m], here)
-            partial(t, first + n, here)
-            return carry
-        lax.fori_loop(0, count, one, 0)
+    def keep(t, at, value):
+        dx, dy, k = ORDER[at]
+        value = low(value)
+        if k == 0:
+            pa[t, 2 * dx + dy, 0:B, :] = value
+        elif k == 1:
+            pa[t, 2 * dx + dy, B:RA, :] = value[:S]
+            pb[t, at, S:B, :] = value[S:]
+        else:
+            pb[t, at] = value
+
+    def partials(t, first, count):
+        for at in range(first, first + count):
+            dx, dy, k = ORDER[at]
+            here = slot(dx, dy, c, k)
+            keep(t, at, half_product(t, here, 0) + half_product(t, here, 1))
+
+    def rows_of(k):
+        return pl.ds(S, B - S) if k == 1 else pl.ds(0, B)
 
     def p(t, dx, dy, k):
-        return pb.at[t, PLACE[(dx, dy, k)]]
+        return pb.at[t, PLACE[(dx, dy, k)], rows_of(k)]
+
+    def first(t, dx, dy):
+        return pa.at[t, 2 * dx + dy]
 
     side = ((xr, 1, xl), (xl, 3, xr))
     land = (froml, fromr)
-    halves = (pl.ds(0, H), pl.ds(H, H))
+    halves = (pl.ds(0, R0), pl.ds(R0, RA - R0))
+    heads = (pl.ds(0, R0), pl.ds(0, RA - R0))
     land_a = (fromla, fromra)
 
     def reduce_blocks(t, between):
         def start(dy):
             for way in range(2):
-                send(("s1", t, way, dy), p(t, 2, dy, 1 + way), fwdb.at[t, way, dy], side[way][0])
+                k = 1 + way
+                send(("s1", t, way, dy), p(t, 2, dy, k), fwdb.at[t, way, dy, rows_of(k)], side[way][0])
 
         def near(dy):
             for way in range(2):
                 k = 2 - way
-                send(("in", t, way, dy), p(t, side[way][1], dy, k), land[way].at[t, dy, k - 1], side[way][0])
+                send(
+                    ("in", t, way, dy), p(t, side[way][1], dy, k),
+                    land[way].at[t, dy, k - 1, rows_of(k)], side[way][0],
+                )
 
         def across(dx):
-            send(("a1", t, dx), p(t, dx, 1, 0), ya.at[t, dx], yp)
+            send(("a1", t, dx), first(t, dx, 1), ya.at[t, dx], yp)
 
         def pass_on(dy):
             for way in range(2):
                 k = 1 + way
-                arrived(("s1", t, way, dy), fwdb.at[t, way, dy], side[way][2])
+                came = fwdb.at[t, way, dy, rows_of(k)]
+                arrived(("s1", t, way, dy), came, side[way][2])
                 mine = p(t, side[way][1], dy, k)
-                mine[...] = low(mine[...].astype(F32) + fwdb[t, way, dy].astype(F32))
-                send(("de", t, way, dy), mine, land[way].at[t, dy, k - 1], side[way][0])
+                mine[...] = low(mine[...].astype(F32) + came[...].astype(F32))
+                send(("de", t, way, dy), mine, land[way].at[t, dy, k - 1, rows_of(k)], side[way][0])
 
         def add_y(dx):
             arrived(("a1", t, dx), ya.at[t, dx], yp)
-            return p(t, dx, 0, 0)[...].astype(F32) + ya[t, dx].astype(F32)
+            return first(t, dx, 0)[...].astype(F32) + ya[t, dx].astype(F32)
 
         for m, (dx, dy, k) in enumerate(ORDER[:2]):
-            pb[t, m] = low(gbuf[1 + m] + half_product(t, slot(dx, dy, c, k), 1))
+            keep(t, m, gbuf[1 + m] + half_product(t, slot(dx, dy, c, k), 1))
         start(1)
         partials(t, 2, 1)
         across(2)
         partials(t, 3, 2)
         start(0)
-        partials(t, 5, 3)
-        for dx in (1, 3, 0):
-            across(dx)
-        partials(t, 8, 4)
+        partials(t, 5, 2)
+        across(1)
+        partials(t, 7, 2)
+        across(3)
+        partials(t, 9, 1)
         near(1)
-        for first in (12, 16, 20):
-            partials(t, first, 4, looped=True)
+        partials(t, 10, 2)
+        across(0)
+        partials(t, 12, 12)
         between()
         pass_on(1)
-        p(t, 2, 0, 0)[...] = low(add_y(2))
+        first(t, 2, 0)[...] = low(add_y(2))
         for way in range(2):
-            send(("fa", t, way), p(t, 2, 0, 0).at[halves[way]], fwda.at[t, way], side[way][0])
+            send(("fa", t, way), first(t, 2, 0).at[halves[way]], fwda.at[t, way, heads[way]], side[way][0])
         near(0)
         pass_on(0)
         for way in range(2):
             dx = side[way][1]
-            p(t, dx, 0, 0)[...] = low(add_y(dx))
-            send(("ia", t, way), p(t, dx, 0, 0).at[halves[1 - way]], land_a[way].at[t, 1 - way], side[way][0])
-        gbuf[0] = add_y(0)
-        for k in (1, 2):
+            first(t, dx, 0)[...] = low(add_y(dx))
+            half = halves[1 - way]
+            send(("ia", t, way), first(t, dx, 0).at[half], land_a[way].at[t, half], side[way][0])
+        ga[...] = add_y(0)
+        for k in (2, 1):
             p(t, 0, 1, k)[...] = low(summed(t, 1, k))
-            send(("b2", t, k), p(t, 0, 1, k), yb.at[t, k - 1], yp)
+            send(("b2", t, k), p(t, 0, 1, k), yb.at[t, k - 1, rows_of(k)], yp)
         for way in range(2):
-            arrived(("fa", t, way), fwda.at[t, way], side[way][2])
-            mine = p(t, side[way][1], 0, 0).at[halves[way]]
-            mine[...] = low(mine[...].astype(F32) + fwda[t, way].astype(F32))
-            send(("da", t, way), mine, land_a[way].at[t, way], side[way][0])
+            came = fwda.at[t, way, heads[way]]
+            arrived(("fa", t, way), came, side[way][2])
+            mine = first(t, side[way][1], 0).at[halves[way]]
+            mine[...] = low(mine[...].astype(F32) + came[...].astype(F32))
+            send(("da", t, way), mine, land_a[way].at[t, halves[way]], side[way][0])
 
     def summed(t, dy, k):
+        value = p(t, 0, dy, k)[...].astype(F32)
         for way in range(2):
             kind = "de" if k == 1 + way else "in"
-            arrived((kind, t, way, dy), land[way].at[t, dy, k - 1], side[way][2])
-        return (
-            p(t, 0, dy, k)[...].astype(F32)
-            + froml[t, dy, k - 1].astype(F32) + fromr[t, dy, k - 1].astype(F32)
-        )
-
-    def finish_sum(t, k):
-        if k > 0:
-            value = summed(t, 0, k)
-            arrived(("b2", t, k), yb.at[t, k - 1], yp)
-            gbuf[k] = value + yb[t, k - 1].astype(F32)
-            return
+            came = land[way].at[t, dy, k - 1, rows_of(k)]
+            arrived((kind, t, way, dy), came, side[way][2])
+            value = value + came[...].astype(F32)
+        return value
+
+    def finish_second(t, k):
+        value = summed(t, 0, k)
+        came = yb.at[t, k - 1, rows_of(k)]
+        arrived(("b2", t, k), came, yp)
+        gbuf[k, S if k == 1 else 0:B, :] = value + came[...].astype(F32)
+
+    def finish_first(t):
         for way in range(2):
-            arrived(("ia", t, way), land_a[way].at[t, 1 - way], side[way][2])
-            arrived(("da", t, way), land_a[way].at[t, way], side[way][2])
-        for half in range(2):
-            rows = slice(half * H, (half + 1) * H)
-            gbuf[0, rows, :] += fromla[t, half].astype(F32) + fromra[t, half].astype(F32)
+            for kind, half in (("ia", halves[1 - way]), ("da", halves[way])):
+                arrived((kind, t, way), land_a[way].at[t, half], side[way][2])
+        value = ga[...] + fromla[t].astype(F32) + fromra[t].astype(F32)
+        gbuf[0] = value[:B]
+        gbuf[1, 0:S, :] = value[B:]
 
     def update(k):
         grad = gbuf[k]
@@ -337,79 +356,96 @@
             hits = total(jnp.where(listing[t] == name, F32(1.0), F32(0.0)))
             qbuf[k, e] = jnp.where(hits > 0.5, value, qbuf[k, e])
 
-    def w_at(dx, dy, k):
-        return wg.at[slot(dx, dy, c, k)]
-
-    def share(dx, dy, k):
-        ref = w_at(dx, dy, k)
-        send(("d", dx, dy, k), ref, ref, sib)
+    def w_at(dx, dy, piece):
+        k, begin, rows = PIECES[piece]
+        return wg.at[slot(dx, dy, c, k), pl.ds(begin, rows)]
+
+    def share(dx, dy, piece):
+        ref = w_at(dx, dy, piece)
+        send(("d", dx, dy, piece), ref, ref, sib)
 
     def gather_blocks():
         def ship(name, ref, dev):
             send(name, ref, ref, dev)
 
-        for k in (1, 2, 0):
-            finish_sum(0, k)
+        def spread(piece):
+            ref = w_at(0, 0, piece)
+            ship(("yo", piece), ref, yp)
+            ship(("r", piece), ref, xr)
+            ship(("l", piece), ref, xl)
+            share(0, 0, piece)
+
+        def renew(k):
             wg[slot(0, 0, c, k)] = update(k)
-            ship(("yo", k), w_at(0, 0, k), yp)
-            ship(("r", k), w_at(0, 0, k), xr)
-            ship(("l", k), w_at(0, 0, k), xl)
-            share(0, 0, k)
-        top, bottom = pl.ds(0, H), pl.ds(H, H)
+
+        def expect(name, dx, dy, piece, dev):
+            arrived(name, w_at(dx, dy, piece), dev)
+            share(dx, dy, piece)
+
+        finish_second(0, 2)
+        renew(2)
+        spread("2")
+        finish_second(0, 1)
+        finish_first(0)
+        renew(1)
+        spread("1b")
+        renew(0)
+        spread("0")
+        spread("1a")
+        refresh(0, (2,))
+        expect(("r", "2"), 3, 0, "2", xl)
+        expect(("l", "2"), 1, 0, "2", xr)
         refresh(0, (1,))
-        arrived(("r", 1), w_at(3, 0, 1), xl)
-        share(3, 0, 1)
-        arrived(("l", 1), w_at(1, 0, 1), xr)
-        share(1, 0, 1)
-        refresh(0, (2,))
-        for k in (1, 2):
-            arrived(("yo", k), w_at(0, 1, k), yp)
-            ship(("rp", k), w_at(0, 1, k), xr)
-            ship(("lp", k), w_at(0, 1, k), xl)
-            share(0, 1, k)
-        arrived(("r", 2), w_at(3, 0, 2), xl)
-        share(3, 0, 2)
-        arrived(("l", 2), w_at(1, 0, 2), xr)
-        share(1, 0, 2)
-        arrived(("r", 0), w_at(3, 0, 0), xl)
-        ship("rh", w_at(3, 0, 0).at[top], xr)
-        ship(("ya", "L"), w_at(3, 0, 0), yp)
-        share(3, 0, 0)
-        arrived(("l", 0), w_at(1, 0, 0), xr)
-        ship("lh", w_at(1, 0, 0).at[bottom], xl)
-        ship(("ya", "R"), w_at(1, 0, 0), yp)
-        share(1, 0, 0)
-        ship(("rf", 0), w_at(3, 0, 1), xr)
-        ship(("lf", 0), w_at(1, 0, 2), xl)
+        for piece in ("2", "1b"):
+            expect(("yo", piece), 0, 1, piece, yp)
+            ship(("rp", piece), w_at(0, 1, piece), xr)
+            ship(("lp", piece), w_at(0, 1, piece), xl)
+        expect(("r", "1b"), 3, 0, "1b", xl)
+        expect(("l", "1b"), 1, 0, "1b", xr)
+        top, bottom = pl.ds(0, R0), pl.ds(R0, B - R0)
+        expect(("r", "0"), 3, 0, "0", xl)
+        ship("rh", wg.at[slot(3, 0, c, 0), top], xr)
+        expect(("l", "0"), 1, 0, "0", xr)
+        ship("lh0", wg.at[slot(1, 0, c, 0), bottom], xl)
+        ship(("ya", "L", "0"), w_at(3, 0, "0"), yp)
+        ship(("ya", "R", "0"), w_at(1, 0, "0"), yp)
+        expect(("r", "1a"), 3, 0, "1a", xl)
+        expect(("l", "1a"), 1, 0, "1a", xr)
+        ship("lh1", w_at(1, 0, "1a"), xl)
+        ship(("ya", "L", "1a"), w_at(3, 0, "1a"), yp)
+        ship(("ya", "R", "1a"), w_at(1, 0, "1a"), yp)
+        ship(("rf", 0), w_at(3, 0, "1b"), xr)
+        ship(("lf", 0), w_at(1, 0, "2"), xl)
         refresh(0, (0,))
-        arrived(("yo", 0), w_at(0, 1, 0), yp)
-        share(0, 1, 0)
-        for k in (1, 2):
-            arrived(("rp", k), w_at(3, 1, k), xl)
-            if k == 1:
-                ship(("rf", 1), w_at(3, 1, 1), xr)
-            share(3, 1, k)
-            arrived(("lp", k), w_at(1, 1, k), xr)
-            if k == 2:
-                ship(("lf", 1), w_at(1, 1, 2), xl)
-            share(1, 1, k)
-        arrived(("ya", "L"), w_at(3, 1, 0), yp)
-        share(3, 1, 0)
-        arrived("rh", w_at(2, 0, 0).at[top], xl)
-        arrived("lh", w_at(2, 0, 0).at[bottom], xr)
-        ship(("ya", "F"), w_at(2, 0, 0), yp)
-        share(2, 0, 0)
-        arrived(("ya", "R"), w_at(1, 1, 0), yp)
-        share(1, 1, 0)
+        for piece in ("0", "1a"):
+            expect(("yo", piece), 0, 1, piece, yp)
+        for piece in ("2", "1b"):
+            expect(("rp", piece), 3, 1, piece, xl)
+            if piece == "1b":
+                ship(("rf", 1), w_at(3, 1, piece), xr)
+            expect(("lp", piece), 1, 1, piece, xr)
+            if piece == "2":
+                ship(("lf", 1), w_at(1, 1, piece), xl)
+        expect(("ya", "L", "0"), 3, 1, "0", yp)
+        arrived("rh", wg.at[slot(2, 0, c, 0), top], xl)
+        arrived("lh0", wg.at[slot(2, 0, c, 0), bottom], xr)
+        ship(("ya", "F", "0"), w_at(2, 0, "0"), yp)
+        share(2, 0, "0")
+        expect("lh1", 2, 0, "1a", xr)
+        ship(("ya", "F", "1a"), w_at(2, 0, "1a"), yp)
+        expect(("ya", "R", "0"), 1, 1, "0", yp)
+        expect(("ya", "L", "1a"), 3, 1, "1a", yp)
+        expect(("ya", "R", "1a"), 1, 1, "1a", yp)
         for dy in range(2):
-            arrived(("rf", dy), w_at(2, dy, 1), xl)
-            share(2, dy, 1)
-            arrived(("lf", dy), w_at(2, dy, 2), xr)
-            share(2, dy, 2)
-        arrived(("ya", "F"), w_at(2, 1, 0), yp)
-        share(2, 1, 0)
-        for dx, dy, k in ORDER:
-            arrived(("d", dx, dy, k), wg.at[slot(dx, dy, 1 - c, k)], sib)
+            expect(("rf", dy), 2, dy, "1b", xl)
+            expect(("lf", dy), 2, dy, "2", xr)
+        for piece in ("0", "1a"):
+            expect(("ya", "F", piece), 2, 1, piece, yp)
+        for dx in range(XN):
+            for dy in range(2):
+                for piece, (k, begin, rows) in PIECES.items():
+                    ref = wg.at[slot(dx, dy, 1 - c, k), pl.ds(begin, rows)]
+                    arrived(("d", dx, dy, piece), ref, sib)
 
     load_x[0].wait()
     load_a.wait()
@@ -440,14 +476,19 @@
     gate(1, lambda j: None, lambda i, j: wg[owner[0, i * CB + j]], lambda n: None)
     wait_dgate(1)
     reduce_blocks(1, lambda: None)
-    for ks in ((1, 2), (0,)):
+    def conclude(ks):
         for k in ks:
-            finish_sum(1, k)
             wout[0, k] = update(k)
         refresh(1, ks)
         for k in ks:
             for e in range(2):
                 rout[0, k, e] = qbuf[k, e]
+
+    finish_second(1, 2)
+    conclude((2,))
+    finish_second(1, 1)
+    finish_first(1)
+    conclude((1, 0))
     for copy in started:
         copy.wait_send()
 
@@ -500,19 +541,21 @@
             pltpu.VMEM((CB, tokens, B), BF16),
             pltpu.VMEM((CB, tokens, B), BF16),
             pltpu.VMEM((CB, tokens, B), BF16),
+            pltpu.VMEM((2, 2 * XN, RA, B), BF16),
             pltpu.VMEM((2, len(ORDER)) + block, BF16),
             pltpu.VMEM((RB * CB,) + block, BF16),
             pltpu.VMEM((OWN,) + block, BF16),
+            pltpu.VMEM((RA, B), F32),
             pltpu.VMEM((OWN,) + block, F32),
             pltpu.VMEM((OWN, 2) + block, F32),
             pltpu.VMEM((OWN, 2) + block, BF16),
             pltpu.VMEM((2, 2, 2) + block, BF16),
             pltpu.VMEM((2, 2, 2) + block, BF16),
             pltpu.VMEM((2, 2, 2) + block, BF16),
-            pltpu.VMEM((2, 4) + block, BF16),
-            pltpu.VMEM((2, 2, H, B), BF16),
-            pltpu.VMEM((2, 2, H, B), BF16),
-            pltpu.VMEM((2, 2, H, B), BF16),
+            pltpu.VMEM((2, XN, RA, B), BF16),
+            pltpu.VMEM((2, 2, R0, B), BF16),
+            pltpu.VMEM((2, RA, B), BF16),
+            pltpu.VMEM((2, RA, B), BF16),
             pltpu.VMEM((2, 2) + block, BF16),
             pltpu.SemaphoreType.DMA((len(NAMES),)),
             pltpu.SemaphoreType.DMA((len(NAMES),)),

time: 93.7 us -> 93.2 us (level)
  no operation moved by 1% of the time
where the time goes in v4:
time: 93.2 us; the launch traced here: 93 us
  Pallas kernels  90.7 us (97%)
  other arithmetic  1.5 us (2%)
    pallas_call x1, Pallas kernels, body(): pl.pallas_call(kernel, out_shape=results, in_specs=[scalars, scalars, loc...  88.6 us
    pallas_call x1, Pallas kernels, body(): pl.pallas_call(deliver, out_shape=results, in_specs=[anywhere] * 2, out_s...  2.15 us

profile of v4, /device:TPU:8, one launch (start us, length us, event | category | flops | bytes accessed | tf_op | source)
XLA Modules:
  0.0 93.0 jit_solution(13378579573443310475)
XLA Ops:
  0.7 0.1 select_select_fusion
  0.7 0.7 iota_compare_fusion
  1.4 0.7 select_reduce_fusion.place
  2.1 88.6 %shard_map.89 = (bf16[1,3,256,256]{3,2,1,0:T(8,128)(2,1)}, bf16[1,3,2,256,256]{4,3,2,1,0:T(8,128)(2,1)}) custom-call(s32[3,48]{1,0:T(4,128)} %select_reduce_fusion.place, s32[1,48]{1,0:T(1,128)} %owner.1, s32[2,4,16]{2,1,0:T(4,128)} %bitcast.2, bf16[2,256,2048]{2,1,0:T(8,128)(2,1)} %feat.1, bf16[2,256,1536]{2,1,0:T(8,128)(2,1)} %act.1, ...), custom_call_target="tpu_custom_call" | custom-call | tf_op jit(solution)/shard_map/pallas_call | solution.py:528
  90.7 2.1 %shard_map.90 = (bf16[1,3,256,256]{3,2,1,0:T(8,128)(2,1)}, bf16[1,3,2,256,256]{4,3,2,1,0:T(8,128)(2,1)}) custom-call(bf16[1,3,256,256]{3,2,1,0:T(8,128)(2,1)} %get-tuple-element.4.weights, bf16[1,3,2,256,256]{4,3,2,1,0:T(8,128)(2,1)} %get-tuple-element.5.roots), custom_call_target="tpu_custom_call" | custom-call | tf_op jit(solution)/shard_map/pallas_call | solution.py:568
  (3 shorter events, 0.0 us)

commit v5 on v4

--- a/solution.py
+++ b/solution.py
@@ -313,15 +313,14 @@
         gbuf[0] = value[:B]
         gbuf[1, 0:S, :] = value[B:]
 
-    def update(k):
-        grad = gbuf[k]
-        left = low(dot(qbuf[k, 0], low(grad)))
-        shaped = dot(left, qbuf[k, 1])
-        grad_norm = jnp.sqrt(total(grad * grad) + NORM_EPS)
-        shaped_norm = jnp.sqrt(total(shaped * shaped) + NORM_EPS)
-        value = low(wown[k].astype(F32) - STEP_SIZE * (grad_norm / shaped_norm) * shaped)
-        wown[k] = value
-        return value
+    def update(ks):
+        grads = [gbuf[k] for k in ks]
+        lefts = [low(dot(qbuf[k, 0], low(grad))) for k, grad in zip(ks, grads)]
+        shaped = [dot(left, qbuf[k, 1]) for k, left in zip(ks, lefts)]
+        grad_norms = [jnp.sqrt(total(grad * grad) + NORM_EPS) for grad in grads]
+        shaped_norms = [jnp.sqrt(total(value * value) + NORM_EPS) for value in shaped]
+        for k, value, top, bottom in zip(ks, shaped, grad_norms, shaped_norms):
+            wown[k] = low(wown[k].astype(F32) - STEP_SIZE * (top / bottom) * value)
 
     def refresh(t, owned):
         rows = lax.broadcasted_iota(jnp.int32, (B, B), 0)
@@ -375,21 +374,22 @@
             ship(("l", piece), ref, xl)
             share(0, 0, piece)
 
-        def renew(k):
-            wg[slot(0, 0, c, k)] = update(k)
+        def renew(ks):
+            update(ks)
+            for k in ks:
+                wg[slot(0, 0, c, k)] = wown[k]
 
         def expect(name, dx, dy, piece, dev):
             arrived(name, w_at(dx, dy, piece), dev)
             share(dx, dy, piece)
 
         finish_second(0, 2)
-        renew(2)
+        renew((2,))
         spread("2")
         finish_second(0, 1)
         finish_first(0)
-        renew(1)
+        renew((1, 0))
         spread("1b")
-        renew(0)
         spread("0")
         spread("1a")
         refresh(0, (2,))
@@ -476,19 +476,26 @@
     gate(1, lambda j: None, lambda i, j: wg[owner[0, i * CB + j]], lambda n: None)
     wait_dgate(1)
     reduce_blocks(1, lambda: None)
+    results = []
+
     def conclude(ks):
+        def put(src, dst):
+            results.append(load(CB + 6 + len(results), src, dst))
+
+        update(ks)
         for k in ks:
-            wout[0, k] = update(k)
+            put(wown.at[k], wout.at[0, k])
         refresh(1, ks)
         for k in ks:
-            for e in range(2):
-                rout[0, k, e] = qbuf[k, e]
+            put(qbuf.at[k], rout.at[0, k])
 
     finish_second(1, 2)
     conclude((2,))
     finish_second(1, 1)
     finish_first(1)
     conclude((1, 0))
+    for copy in results:
+        copy.wait()
     for copy in started:
         copy.wait_send()
 
@@ -529,7 +536,7 @@
         kernel,
         out_shape=results,
         in_specs=[scalars, scalars, local] + [anywhere] * 5,
-        out_specs=(local, local),
+        out_specs=(anywhere, anywhere),
         scratch_shapes=[
             pltpu.VMEM((2, tokens, RB * B), BF16),
             pltpu.VMEM((2, tokens, RB * B), BF16),
@@ -559,7 +566,7 @@
             pltpu.VMEM((2, 2) + block, BF16),
             pltpu.SemaphoreType.DMA((len(NAMES),)),
             pltpu.SemaphoreType.DMA((len(NAMES),)),
-            pltpu.SemaphoreType.DMA((16,)),
+            pltpu.SemaphoreType.DMA((CB + 6 + 2 * OWN,)),
         ],
         compiler_params=pltpu.CompilerParams(
             collective_id=0, has_side_effects=True, vmem_limit_bytes=60 * 1024 * 1024

time: 93.2 us -> 93.6 us (level)
  no operation moved by 1% of the time
where the time goes in v5:
time: 93.6 us; the launch traced here: 93.5 us
  Pallas kernels  91.2 us (97%)
  other arithmetic  1.5 us (2%)
    pallas_call x1, Pallas kernels, body(): pl.pallas_call(kernel, out_shape=results, in_specs=[scalars, scalars, loc...  89 us
    pallas_call x1, Pallas kernels, body(): pl.pallas_call(deliver, out_shape=results, in_specs=[anywhere] * 2, out_s...  2.15 us

profile of v5, /device:TPU:8, one launch (start us, length us, event | category | flops | bytes accessed | tf_op | source)
XLA Modules:
  0.0 93.5 jit_solution(14011007541356485882)
XLA Ops:
  0.7 0.1 select_select_fusion
  0.7 0.7 iota_compare_fusion
  1.4 0.7 select_reduce_fusion.place
  2.1 89.0 %shard_map.89 = (bf16[1,3,256,256]{3,2,1,0:T(8,128)(2,1)}, bf16[1,3,2,256,256]{4,3,2,1,0:T(8,128)(2,1)}) custom-call(s32[3,48]{1,0:T(4,128)} %select_reduce_fusion.place, s32[1,48]{1,0:T(1,128)} %owner.1, s32[2,4,16]{2,1,0:T(4,128)} %bitcast.2, bf16[2,256,2048]{2,1,0:T(8,128)(2,1)} %feat.1, bf16[2,256,1536]{2,1,0:T(8,128)(2,1)} %act.1, ...), custom_call_target="tpu_custom_call" | custom-call | tf_op jit(solution)/shard_map/pallas_call | solution.py:535
  91.2 2.1 %shard_map.90 = (bf16[1,3,256,256]{3,2,1,0:T(8,128)(2,1)}, bf16[1,3,2,256,256]{4,3,2,1,0:T(8,128)(2,1)}) custom-call(bf16[1,3,256,256]{3,2,1,0:T(8,128)(2,1)} %get-tuple-element.4.weights, bf16[1,3,2,256,256]{4,3,2,1,0:T(8,128)(2,1)} %get-tuple-element.5.roots), custom_call_target="tpu_custom_call" | custom-call | tf_op jit(solution)/shard_map/pallas_call | solution.py:575
  (3 shorter events, 0.0 us)

commit v6 on v5

--- a/solution.py
+++ b/solution.py
@@ -267,8 +267,8 @@
         partials(t, 10, 2)
         across(0)
         partials(t, 12, 12)
+        pass_on(1)
         between()
-        pass_on(1)
         first(t, 2, 0)[...] = low(add_y(2))
         for way in range(2):
             send(("fa", t, way), first(t, 2, 0).at[halves[way]], fwda.at[t, way, heads[way]], side[way][0])

time: 93.6 us -> 93.6 us (level)
  no operation moved by 1% of the time
where the time goes in v6:
time: 93.6 us; the launch traced here: 93.5 us
  Pallas kernels  91.2 us (97%)
  other arithmetic  1.5 us (2%)
    pallas_call x1, Pallas kernels, body(): pl.pallas_call(kernel, out_shape=results, in_specs=[scalars, scalars, loc...  89 us
    pallas_call x1, Pallas kernels, body(): pl.pallas_call(deliver, out_shape=results, in_specs=[anywhere] * 2, out_s...  2.15 us

profile of v6, /device:TPU:8, one launch (start us, length us, event | category | flops | bytes accessed | tf_op | source)
XLA Modules:
  0.0 93.5 jit_solution(1349057217886054453)
XLA Ops:
  0.7 0.1 select_select_fusion
  0.7 0.7 iota_compare_fusion
  1.4 0.7 select_reduce_fusion.place
  2.1 89.0 %shard_map.89 = (bf16[1,3,256,256]{3,2,1,0:T(8,128)(2,1)}, bf16[1,3,2,256,256]{4,3,2,1,0:T(8,128)(2,1)}) custom-call(s32[3,48]{1,0:T(4,128)} %select_reduce_fusion.place, s32[1,48]{1,0:T(1,128)} %owner.1, s32[2,4,16]{2,1,0:T(4,128)} %bitcast.2, bf16[2,256,2048]{2,1,0:T(8,128)(2,1)} %feat.1, bf16[2,256,1536]{2,1,0:T(8,128)(2,1)} %act.1, ...), custom_call_target="tpu_custom_call" | custom-call | tf_op jit(solution)/shard_map/pallas_call | solution.py:535
  91.2 2.1 %shard_map.90 = (bf16[1,3,256,256]{3,2,1,0:T(8,128)(2,1)}, bf16[1,3,2,256,256]{4,3,2,1,0:T(8,128)(2,1)}) custom-call(bf16[1,3,256,256]{3,2,1,0:T(8,128)(2,1)} %get-tuple-element.4.weights, bf16[1,3,2,256,256]{4,3,2,1,0:T(8,128)(2,1)} %get-tuple-element.5.roots), custom_call_target="tpu_custom_call" | custom-call | tf_op jit(solution)/shard_map/pallas_call | solution.py:575
  (3 shorter events, 0.0 us)
